TPU v7x, 8 devices: a whole 2x2x1 slice. The times are simulated.
8 devices in a mesh: dp: 1 (over z), tp: 2 (over y), sp: 4 (over x, core).
Axes of the slice: x: 2, y: 2, z: 1, core: 2. Of those that a mesh axis runs over, the one named last changes fastest.
Arguments:
- hidden: bfloat16 [64, 4096], P('dp')
- positions: int32 [64], P('dp')
- k_cache: bfloat16 [2, 64, 512, 8, 128], P(None, 'dp', 'sp', 'tp')
- v_cache: bfloat16 [2, 64, 512, 8, 128], P(None, 'dp', 'sp', 'tp')
- ln_gain: bfloat16 [2, 2, 4096], replicated
- ln_bias: bfloat16 [2, 2, 4096], replicated
- w_qkv: bfloat16 [2, 4096, 6144], P(None, None, 'tp')
- b_qkv: bfloat16 [2, 6144], P(None, 'tp')
- w_dense: bfloat16 [2, 4096, 4096], P(None, 'tp')
- b_dense: bfloat16 [2, 4096], replicated
- w_up: bfloat16 [2, 4096, 28672], P(None, None, 'tp')
- b_up: bfloat16 [2, 28672], P(None, 'tp')
- w_down: bfloat16 [2, 14336, 4096], P(None, 'tp')
- b_down: bfloat16 [2, 4096], replicated
Outputs:
- output 1: bfloat16 [64, 4096], P('dp')
- output 2: bfloat16 [2, 64, 512, 8, 128], P(None, 'dp', 'sp', 'tp')
- output 3: bfloat16 [2, 64, 512, 8, 128], P(None, 'dp', 'sp', 'tp')
All inputs are finite; a program needn't handle non-finite values.
Results may differ from a plain program's by a relative error of at most 0.0172843.
Values sent between devices are 32-bit elements.
A program may use at most 2 GiB of HBM per device.

v0:
```python
import jax
import jax.numpy as jnp
from jax import lax
from jax.sharding import PartitionSpec as P

BLOCK_SIZE = 64
LOCAL_BLOCKS = 16
VERT_STRIDE = 8
ROPE_THETA = 1000000.0
GELU_LIMIT = 20.0
NORM_EPS = 0.00001
MASKED = -1e30


def layer_norm(vec, gain, shift):
    wide_vec = vec.astype(jnp.float32)
    mean_val = jnp.mean(wide_vec, axis=-1, keepdims=True)
    variance = jnp.mean(jnp.square(wide_vec - mean_val), axis=-1, keepdims=True)
    normed = (wide_vec - mean_val) * lax.rsqrt(variance + NORM_EPS)
    return (normed * gain.astype(jnp.float32) + shift.astype(jnp.float32)).astype(jnp.bfloat16)


def rotary(col_pairs, positions):
    head_dim = col_pairs.shape[-1]
    half_dim = head_dim // 2
    inv_freq = ROPE_THETA ** (-jnp.arange(half_dim).astype(jnp.float32) * (2.0 / head_dim))
    angles = positions.astype(jnp.float32)[:, None] * inv_freq[None, :]
    cos_part = jnp.cos(angles)[:, None, None, :]
    sin_part = jnp.sin(angles)[:, None, None, :]
    first_half = col_pairs[..., :half_dim]
    second_half = col_pairs[..., half_dim:]
    return jnp.concatenate([first_half * cos_part - second_half * sin_part, second_half * cos_part + first_half * sin_part], axis=-1)


def gegelu(up_proj):
    col_pairs = up_proj.reshape(up_proj.shape[0], -1, 2)
    gate_part = jnp.minimum(col_pairs[..., 0], GELU_LIMIT)
    linear_part = jnp.clip(col_pairs[..., 1], -GELU_LIMIT, GELU_LIMIT)
    return gate_part * jax.nn.sigmoid(1.702 * gate_part) * (linear_part + 1.0)


def project_qkv(hidden, positions, gain, shift, w_qkv, b_qkv, kv_count, head_dim):
    normed = layer_norm(hidden, gain, shift)
    qkv_proj = jnp.dot(normed, w_qkv, preferred_element_type=jnp.float32) + b_qkv.astype(jnp.float32)
    qkv_proj = qkv_proj.reshape(hidden.shape[0], kv_count, -1, head_dim)
    group_size = qkv_proj.shape[2] - 2
    turned = rotary(qkv_proj[:, :, :group_size + 1], positions)
    query_rot = turned[:, :, :group_size].astype(jnp.bfloat16)
    k_new = turned[:, :, group_size].astype(jnp.bfloat16)
    v_new = qkv_proj[:, :, group_size + 1].astype(jnp.bfloat16)
    return query_rot, k_new, v_new


def keep_mask(slot_ids, positions, head_ids, sparse):
    causal = (slot_ids[None, :] <= positions[:, None])[:, None, None, :]
    if not sparse:
        return causal
    blocks = slot_ids // BLOCK_SIZE
    near_mask = (positions[:, None] // BLOCK_SIZE - blocks[None, :]) < LOCAL_BLOCKS
    vertical = (blocks[None, None, :] + head_ids[:, :, None] + 1) % VERT_STRIDE == 0
    return causal & (near_mask[:, None, None, :] | vertical[None])


def partial_attention(query_rot, key_rows, value_rows, attn_mask):
    scores = jnp.einsum('bkgd,btkd->bkgt', query_rot, key_rows, preferred_element_type=jnp.float32) / query_rot.shape[-1]
    scores = jnp.where(attn_mask, scores, MASKED)
    peak_score = jnp.max(scores, axis=-1)
    weights = jnp.where(attn_mask, jnp.exp(scores - peak_score[..., None]), 0.0)
    weight_sum = jnp.sum(weights, axis=-1)
    mixed_vals = jnp.einsum('bkgt,btkd->bkgd', weights.astype(jnp.bfloat16), value_rows, preferred_element_type=jnp.float32)
    return peak_score, weight_sum, mixed_vals


def combine_shards(peak_score, weight_sum, mixed_vals):
    head_dim = mixed_vals.shape[-1]
    packed = jnp.concatenate([mixed_vals, peak_score[..., None], weight_sum[..., None]], axis=-1)
    gathered = lax.all_gather(packed, 'sp')
    peaks = gathered[..., head_dim]
    top_peak = jnp.max(peaks, axis=0)
    rescale = jnp.exp(peaks - top_peak[None])
    numerator = jnp.sum(gathered[..., :head_dim] * rescale[..., None], axis=0)
    denominator = jnp.sum(gathered[..., head_dim + 1] * rescale, axis=0)
    return (numerator / denominator[..., None]).astype(jnp.bfloat16)


def finish_layer(hidden, attn_part, gains, shifts, b_dense, w_up, b_up, w_down, b_down):
    attn_proj = lax.psum(attn_part, 'tp')
    residual = (hidden.astype(jnp.float32) + attn_proj + b_dense.astype(jnp.float32)).astype(jnp.bfloat16)
    normed = layer_norm(residual, gains[1], shifts[1])
    up_proj = jnp.dot(normed, w_up, preferred_element_type=jnp.float32) + b_up.astype(jnp.float32)
    gated = gegelu(up_proj).astype(jnp.bfloat16)
    down_proj = lax.psum(jnp.dot(gated, w_down, preferred_element_type=jnp.float32), 'tp')
    return (residual.astype(jnp.float32) + down_proj + b_down.astype(jnp.float32)).astype(jnp.bfloat16)


def solution(mesh):
    cache_spec = P(None, 'dp', 'sp', 'tp', None)
    in_specs = (P('dp', None), P('dp'), cache_spec, cache_spec, P(), P(), P(None, None, 'tp'), P(None, 'tp'), P(None, 'tp', None), P(), P(None, None, 'tp'), P(None, 'tp'), P(None, 'tp', None), P())
    out_specs = (P('dp', None), cache_spec, cache_spec)

    def device_step(hidden, positions, k_cache, v_cache, ln_gain, ln_bias, w_qkv, b_qkv, w_dense, b_dense, w_up, b_up, w_down, b_down):
        tp_index = lax.axis_index('tp')
        sp_index = lax.axis_index('sp')
        num_seqs = hidden.shape[0]
        slots_local = k_cache.shape[2]
        kv_local = k_cache.shape[3]
        head_dim = k_cache.shape[4]
        slot_ids = sp_index * slots_local + jnp.arange(slots_local)
        hit_mask = (slot_ids[None, :] == positions[:, None])[:, :, None, None]
        k_layers = []
        v_layers = []
        for layer_idx in range(2):
            query_rot, k_new, v_new = project_qkv(hidden, positions, ln_gain[layer_idx, 0], ln_bias[layer_idx, 0], w_qkv[layer_idx], b_qkv[layer_idx], kv_local, head_dim)
            group_size = query_rot.shape[2]
            key_rows = jnp.where(hit_mask, k_new[:, None], k_cache[layer_idx])
            value_rows = jnp.where(hit_mask, v_new[:, None], v_cache[layer_idx])
            head_ids = (tp_index * kv_local * group_size + jnp.arange(kv_local * group_size)).reshape(kv_local, group_size)
            attn_mask = keep_mask(slot_ids, positions, head_ids, layer_idx == 0)
            peak_score, weight_sum, mixed_vals = partial_attention(query_rot, key_rows, value_rows, attn_mask)
            attn_out = combine_shards(peak_score, weight_sum, mixed_vals)
            attn_part = jnp.dot(attn_out.reshape(num_seqs, -1), w_dense[layer_idx], preferred_element_type=jnp.float32)
            hidden = finish_layer(hidden, attn_part, ln_gain[layer_idx], ln_bias[layer_idx], b_dense[layer_idx], w_up[layer_idx], b_up[layer_idx], w_down[layer_idx], b_down[layer_idx])
            k_layers.append(key_rows)
            v_layers.append(value_rows)
        return hidden, jnp.stack(k_layers), jnp.stack(v_layers)

    return jax.shard_map(device_step, mesh=mesh, in_specs=in_specs, out_specs=out_specs, check_vma=False)
```

profile of v0, /device:TPU:0, one launch (start us, length us, event | category | flops | bytes accessed | tf_op | source)
XLA Modules:
  0.0 556.1 jit_solution(175029059974623744)
XLA Ops:
  14.3 10.7 %fusion.38 = f32[64,3072]{1,0:T(8,128)S(1)} fusion(bf16[2,4096,3072]{2,1,0:T(8,128)(2,1)} %param.20, bf16[64,4096]{1,0:T(8,128)(2,1)} %param.14, f32[4096]{0:T(1024)S(1)} %bitcast.139, f32[4096]{0:T(1024)S(1)} %bitcast.138, f32[64]{0:T(128)S(1)} %add_rsqrt_fusion.3, f32[64]{0:T(128)S(1)} %broadcast_multiply_fusion.3, f32[3072]{0:T(1024)S(1)} %bitcast.141), kind=kOutput, calls=%fused_computation.46 | convolution fusion | flops 1612382208 | bytes 26522112 | tf_op jit(solution)/shard_map/dot_general | solution.py:44
  27.6 12.9 %bitcast_select_fusion.2 = (bf16[64,128,4,128]{3,2,1,0:T(4,128)(2,1)S(1)}, bf16[64,128,4,128]{3,2,1,0:T(4,128)(2,1)S(1)}) fusion(pred[64,128]{1,0:T(8,128)(4,1)S(1)} %get-tuple-element.50, bf16[2,64,128,4,128]{4,3,2,1,0:T(4,128)(2,1)} %param.17, bf16[64,4,128]{2,1,0:T(4,128)(2,1)S(1)} %copy.163, bf16[2,64,128,4,128]{4,3,2,1,0:T(4,128)(2,1)} %param.16, ...), kind=kLoop, calls=%fused_computation.30 | loop fusion | flops 8388608 | bytes 33693696 | tf_op jit(solution)/shard_map/jit(_where)/select_n | solution.py:116
  53.4 34.1 %all-gather.5.cloned.1.call-done = f32[256,4,4,130]{3,2,1,0:T(4,128)} async-done(((f32[64,4,4,130]{3,2,1,0:T(4,128)}), f32[256,4,4,130]{3,2,1,0:T(4,128)}) %all-gather.5.cloned.1.call-update) | async-done | bytes 2129936 | tf_op jit(solution)/shard_map/all_gather | solution.py:77
  108.1 8.4 %fusion.20 = f32[64,4096]{1,0:T(8,128)} fusion(bf16[64,2048]{0,1:T(8,128)(2,1)S(1)} %bitcast.116, bf16[2,2048,4096]{2,1,0:T(8,128)(2,1)} %param.22), kind=kOutput, calls=%fused_computation.22 | convolution fusion | flops 1073741824 | bytes 18087936 | tf_op jit(solution)/shard_map/dot_general | solution.py:121
  118.0 33.0 %all-reduce.5.cloned.1.call-done = f32[64,4096]{1,0:T(8,128)} async-done(((f32[64,4096]{1,0:T(8,128)}), f32[64,4096]{1,0:T(8,128)}) %all-reduce.5.cloned.1.call-update) | async-done | bytes 1048592 | tf_op jit(solution)/shard_map/psum | solution.py:87
  152.8 39.6 %fusion.24 = f32[64,14336]{1,0:T(8,128)} fusion(bf16[2,4096,14336]{2,1,0:T(8,128)(2,1)} %param.24, f32[14336]{0:T(1024)S(1)} %bitcast.131, bf16[64,4096]{1,0:T(8,128)(2,1)S(1)} %get-tuple-element.8, f32[4096]{0:T(1024)S(1)} %bitcast.137, f32[4096]{0:T(1024)S(1)} %bitcast.136, f32[64]{0:T(128)S(1)} %add_rsqrt_fusion.2, f32[64]{0:T(128)S(1)} %broadcast_multiply_fusion.2), kind=kOutput, calls=%fused_computation.26 | convolution fusion | flops 7518683136 | bytes 121725440 | tf_op jit(solution)/shard_map/dot_general | solution.py:90
  198.7 10.4 %fusion.148 = (f32[64,7168,1]{0,2,1:T(1,128)}, f32[64,7168,1]{0,2,1:T(1,128)}) fusion(f32[64,7168,2]{0,2,1:T(2,128)} %bitcast.110), kind=kLoop, calls=%fused_computation.220 | loop fusion | bytes 7340032 | tf_op jit(solution)/shard_map/slice | solution.py:37
  209.1 7.2 %copy.214 = f32[64,7168,1]{1,0,2:T(8,128)S(1)} copy(f32[64,7168,1]{0,2,1:T(1,128)} %get-tuple-element.15) | data formatting | bytes 3670016
  216.3 8.3 %copy.215 = f32[64,7168,1]{1,0,2:T(8,128)} copy(f32[64,7168,1]{0,2,1:T(1,128)} %get-tuple-element.16) | data formatting | bytes 3670016
  224.7 22.2 %fusion.8 = f32[64,4096]{1,0:T(8,128)} fusion(bf16[2,7168,4096]{2,1,0:T(8,128)(2,1)} %param.26, f32[64,7168,1]{1,0,2:T(8,128)} %copy.215, f32[64,7168,1]{1,0,2:T(8,128)S(1)} %copy.214), kind=kOutput, calls=%fused_computation.8 | convolution fusion | flops 3762683904 | bytes 63438848 | tf_op jit(solution)/shard_map/dot_general | solution.py:92
  247.8 33.6 %all-reduce.7.cloned.1.call-done = f32[64,4096]{1,0:T(8,128)} async-done(((f32[64,4096]{1,0:T(8,128)}), f32[64,4096]{1,0:T(8,128)}) %all-reduce.7.cloned.1.call-update) | async-done | bytes 1048592 | tf_op jit(solution)/shard_map/psum | solution.py:92
  283.2 10.6 %fusion.41 = f32[64,3072]{1,0:T(8,128)S(1)} fusion(bf16[2,4096,3072]{2,1,0:T(8,128)(2,1)} %param.20, bf16[64,4096]{1,0:T(8,128)(2,1)S(1)} %get-tuple-element.6, f32[4096]{0:T(1024)S(1)} %bitcast.135, f32[4096]{0:T(1024)S(1)} %bitcast.134, f32[64]{0:T(128)S(1)} %add_rsqrt_fusion.1, f32[64]{0:T(128)S(1)} %broadcast_multiply_fusion.1, f32[3072]{0:T(1024)S(1)} %bitcast.140), kind=kOutput, calls=%fused_computation.47 | convolution fusion | flops 1612382208 | bytes 26522112 | tf_op jit(solution)/shard_map/dot_general | solution.py:44
  295.8 13.0 %bitcast_select_fusion = (bf16[64,128,4,128]{3,2,1,0:T(4,128)(2,1)S(1)}, bf16[64,128,4,128]{3,2,1,0:T(4,128)(2,1)S(1)}) fusion(pred[64,128]{1,0:T(8,128)(4,1)S(1)} %get-tuple-element.50, bf16[2,64,128,4,128]{4,3,2,1,0:T(4,128)(2,1)} %param.17, bf16[64,4,128]{2,1,0:T(4,128)(2,1)S(1)} %copy.180, bf16[2,64,128,4,128]{4,3,2,1,0:T(4,128)(2,1)} %param.16, ...), kind=kLoop, calls=%fused_computation.28 | loop fusion | flops 8388608 | bytes 33693696 | tf_op jit(solution)/shard_map/jit(_where)/select_n | solution.py:116
  321.5 22.7 %broadcast_select_fusion.1 = (bf16[1,64,128,4,128]{4,3,2,1,0:T(4,128)(2,1)}, bf16[1,64,128,4,128]{4,3,2,1,0:T(4,128)(2,1)}, bf16[1,64,128,4,128]{4,3,2,1,0:T(4,128)(2,1)}, bf16[1,64,128,4,128]{4,3,2,1,0:T(4,128)(2,1)}) fusion(pred[64,128]{1,0:T(8,128)(4,1)S(1)} %get-tuple-element.50, bf16[2,64,128,4,128]{4,3,2,1,0:T(4,128)(2,1)} %param.17, ...), kind=kLoop, calls=%fused_computation.41 | loop fusion | flops 16777216 | bytes 67379200 | tf_op jit(solution)/shard_map/jit(_where)/select_n | solution.py:116
  344.3 8.7 %all-gather.7.cloned.1.call-done = f32[256,4,4,130]{3,2,1,0:T(4,128)} async-done(((f32[64,4,4,130]{3,2,1,0:T(4,128)}), f32[256,4,4,130]{3,2,1,0:T(4,128)}) %all-gather.7.cloned.1.call-update) | async-done | bytes 2129936 | tf_op jit(solution)/shard_map/all_gather | solution.py:77
  373.6 8.4 %fusion.18 = f32[64,4096]{1,0:T(8,128)} fusion(bf16[64,2048]{0,1:T(8,128)(2,1)S(1)} %bitcast.117, bf16[2,2048,4096]{2,1,0:T(8,128)(2,1)} %param.22), kind=kOutput, calls=%fused_computation.20 | convolution fusion | flops 1073741824 | bytes 18087936 | tf_op jit(solution)/shard_map/dot_general | solution.py:121
  382.3 15.1 %pad_maximum_fusion.1 = bf16[2,64,128,4,128]{4,3,2,1,0:T(4,128)(2,1)} fusion(bf16[1,64,128,4,128]{4,3,2,1,0:T(4,128)(2,1)} %get-tuple-element.10, bf16[1,64,128,4,128]{4,3,2,1,0:T(4,128)(2,1)} %get-tuple-element.9), kind=kLoop, calls=%fused_computation.19 | loop fusion | flops 8388608 | bytes 33554432 | tf_op jit(solution)/shard_map/stack | solution.py:125
  397.5 18.9 %all-reduce.9.cloned.1.call-done = f32[64,4096]{1,0:T(8,128)} async-done(((f32[64,4096]{1,0:T(8,128)}), f32[64,4096]{1,0:T(8,128)}) %all-reduce.9.cloned.1.call-update) | async-done | bytes 1048592 | tf_op jit(solution)/shard_map/psum | solution.py:87
  418.3 39.6 %fusion.27 = f32[64,14336]{1,0:T(8,128)} fusion(bf16[2,4096,14336]{2,1,0:T(8,128)(2,1)} %param.24, f32[14336]{0:T(1024)S(1)} %bitcast.130, bf16[64,4096]{1,0:T(8,128)(2,1)S(1)} %get-tuple-element.4, f32[4096]{0:T(1024)S(1)} %bitcast.133, f32[4096]{0:T(1024)S(1)} %bitcast.132, f32[64]{0:T(128)S(1)} %add_rsqrt_fusion, f32[64]{0:T(128)S(1)} %broadcast_multiply_fusion), kind=kOutput, calls=%fused_computation.27 | convolution fusion | flops 7518683136 | bytes 121725440 | tf_op jit(solution)/shard_map/dot_general | solution.py:90
  464.1 10.3 %fusion.147 = (f32[64,7168,1]{0,2,1:T(1,128)}, f32[64,7168,1]{0,2,1:T(1,128)}) fusion(f32[64,7168,2]{0,2,1:T(2,128)} %bitcast.111), kind=kLoop, calls=%fused_computation.219 | loop fusion | bytes 7340032 | tf_op jit(solution)/shard_map/slice | solution.py:37
  481.6 8.3 %copy.220 = f32[64,7168,1]{1,0,2:T(8,128)} copy(f32[64,7168,1]{0,2,1:T(1,128)} %get-tuple-element.14) | data formatting | bytes 3670016
  490.0 22.3 %fusion.6 = f32[64,4096]{1,0:T(8,128)} fusion(bf16[2,7168,4096]{2,1,0:T(8,128)(2,1)} %param.26, f32[64,7168,1]{1,0,2:T(8,128)} %copy.220, f32[64,7168,1]{1,0,2:T(8,128)S(1)} %copy.219), kind=kOutput, calls=%fused_computation.6 | convolution fusion | flops 3762683904 | bytes 63438848 | tf_op jit(solution)/shard_map/dot_general | solution.py:92
  512.3 15.1 %pad_maximum_fusion = bf16[2,64,128,4,128]{4,3,2,1,0:T(4,128)(2,1)} fusion(bf16[1,64,128,4,128]{4,3,2,1,0:T(4,128)(2,1)} %get-tuple-element.43, bf16[1,64,128,4,128]{4,3,2,1,0:T(4,128)(2,1)} %get-tuple-element.44), kind=kLoop, calls=%fused_computation.18 | loop fusion | flops 8388608 | bytes 33554432 | tf_op jit(solution)/shard_map/stack | solution.py:125
  527.4 19.3 %all-reduce.11.cloned.1.call-done = f32[64,4096]{1,0:T(8,128)} async-done(((f32[64,4096]{1,0:T(8,128)}), f32[64,4096]{1,0:T(8,128)}) %all-reduce.11.cloned.1.call-update) | async-done | bytes 1048592 | tf_op jit(solution)/shard_map/psum | solution.py:92
  (116 shorter events, 108.3 us)
Async XLA Ops:
  7.2 80.3 %all-gather.5.cloned.1.call-start = ((), (), s32[]{:S(2)}) async-start(), calls=%async_computation.4 | async-start | bytes 5242880 | tf_op jit(solution)/shard_map/all_gather | solution.py:77
  14.3 13.1 %copy-start.9 = (s32[64]{0:T(128)S(1)}, s32[64]{0:T(128)}, u32[]{:S(2)}) copy-start(s32[64]{0:T(128)} %param.15) | copy-start | bytes 772
  53.0 98.0 %all-reduce.5.cloned.1.call-start = ((), (), s32[]{:S(2)}) async-start(), calls=%async_computation | async-start | bytes 2097152 | tf_op jit(solution)/shard_map/psum | solution.py:87
  108.1 8.5 %copy-start.1 = (bf16[2,14336]{1,0:T(2,128)(2,1)S(1)}, bf16[2,14336]{1,0:T(2,128)(2,1)}, u32[]{:S(2)}) copy-start(bf16[2,14336]{1,0:T(2,128)(2,1)} %param.25) | copy-start | bytes 172036
  108.1 9.2 %copy-start.4 = (bf16[2,4096]{1,0:T(2,128)(2,1)S(1)}, bf16[2,4096]{1,0:T(2,128)(2,1)}, u32[]{:S(2)}) copy-start(bf16[2,4096]{1,0:T(2,128)(2,1)} %param.23) | copy-start | bytes 49156
  108.1 42.9 %copy-start = (bf16[64,4096]{1,0:T(8,128)(2,1)S(1)}, bf16[64,4096]{1,0:T(8,128)(2,1)}, u32[]{:S(2)}) copy-start(bf16[64,4096]{1,0:T(8,128)(2,1)} %param.14) | copy-start | bytes 1572868
  116.6 164.8 %all-reduce.7.cloned.1.call-start = ((), (), s32[]{:S(2)}) async-start(), calls=%async_computation.1 | async-start | bytes 2097152 | tf_op jit(solution)/shard_map/psum | solution.py:92
  224.7 22.5 %copy-start.5 = (bf16[2,4096]{1,0:T(2,128)(2,1)S(1)}, bf16[2,4096]{1,0:T(2,128)(2,1)}, u32[]{:S(2)}) copy-start(bf16[2,4096]{1,0:T(2,128)(2,1)} %param.27) | copy-start | bytes 49156
  246.9 106.0 %all-gather.7.cloned.1.call-start = ((), (), s32[]{:S(2)}) async-start(), calls=%async_computation.5 | async-start | bytes 5242880 | tf_op jit(solution)/shard_map/all_gather | solution.py:77
  321.3 95.1 %all-reduce.9.cloned.1.call-start = ((), (), s32[]{:S(2)}) async-start(), calls=%async_computation.2 | async-start | bytes 2097152 | tf_op jit(solution)/shard_map/psum | solution.py:87
  382.0 164.7 %all-reduce.11.cloned.1.call-start = ((), (), s32[]{:S(2)}) async-start(), calls=%async_computation.3 | async-start | bytes 2097152 | tf_op jit(solution)/shard_map/psum | solution.py:92
  382.3 34.1 %copy-start.3 = (f32[1,4096]{1,0:T(1,128)S(1)}, f32[1,4096]{1,0:T(1,128)}, u32[]{:S(2)}) copy-start(f32[1,4096]{1,0:T(1,128)} %get-tuple-element.40) | copy-start | bytes 49156
  382.3 35.9 %copy-start.6 = (f32[1,14336]{1,0:T(1,128)S(1)}, f32[1,14336]{1,0:T(1,128)}, u32[]{:S(2)}) copy-start(f32[1,14336]{1,0:T(1,128)} %get-tuple-element.28) | copy-start | bytes 172036
  382.3 35.9 %copy-start.7 = (f32[1,1,4096]{2,1,0:T(1,128)S(1)}, f32[1,1,4096]{2,1,0:T(1,128)}, u32[]{:S(2)}) copy-start(f32[1,1,4096]{2,1,0:T(1,128)} %get-tuple-element.29) | copy-start | bytes 49156
  382.3 35.9 %copy-start.8 = (f32[1,1,4096]{2,1,0:T(1,128)S(1)}, f32[1,1,4096]{2,1,0:T(1,128)}, u32[]{:S(2)}) copy-start(f32[1,1,4096]{2,1,0:T(1,128)} %get-tuple-element.33) | copy-start | bytes 49156
  512.3 34.4 %copy-start.2 = (f32[1,4096]{1,0:T(1,128)S(1)}, f32[1,4096]{1,0:T(1,128)}, u32[]{:S(2)}) copy-start(f32[1,4096]{1,0:T(1,128)} %get-tuple-element.37) | copy-start | bytes 49156
Sparse Core Ops, SparseCore 0:
  53.1 34.3 all-gather.4
  116.7 34.2 all-reduce.4
  247.1 34.2 all-reduce.6
  321.4 31.4 all-gather.6
  382.1 34.2 all-reduce.8
  512.4 34.2 all-reduce.10
where the time goes:
time: 567 us; the launch traced here: 556 us
  matrix products  176 us (31%)
  waiting for transfers between devices  148 us (26%)
  other arithmetic  126 us (22%)
  local copies, waits for them, and re-layouts  91 us (16%)
  between operations  15.1 us (3%)
    dot_general x2, matrix products, finish_layer(): jnp.dot(normed, w_up, preferred_element_type=jnp.float32)  79.2 us
    psum x2, waiting for transfers between devices, finish_layer(): lax.psum(jnp.dot(gated, w_down, preferred_element_type=jnp.float32), 'tp')  52.9 us
    psum x2, waiting for transfers between devices, finish_layer(): attn_proj = lax.psum(attn_part, 'tp')  52 us
    select_n x3, other arithmetic, device_step(): value_rows = jnp.where(hit_mask, v_new[:, None], v_cache[layer_idx])  48.6 us
    unnamed x32, local copies, waits for them, and re-layouts  45.7 us
    dot_general x2, matrix products, finish_layer(): jnp.dot(gated, w_down, preferred_element_type=jnp.float32)  44.5 us
    all_gather x2, waiting for transfers between devices, combine_shards(): gathered = lax.all_gather(packed, 'sp')  42.7 us
    another operation x2, other arithmetic, device_step(): return (hidden, jnp.stack(k_layers), jnp.stack(v_layers))  30.3 us
  transfers between devices with their start and end apart: 6, of which 6 were waited for; matrix products, arithmetic and copies ran while one was open for 10% of the time, Pallas kernels for 0%

commit v1 on v0

v1 whole, which is shorter than its diff:
```python
import functools

import jax
import jax.numpy as jnp
from jax import lax
from jax.experimental import pallas as pl
from jax.experimental.pallas import tpu as pltpu
from jax.sharding import PartitionSpec as P

BLOCK_SIZE = 64
LOCAL_BLOCKS = 16
VERT_STRIDE = 8
ROPE_THETA = 1000000.0
GELU_LIMIT = 20.0
NORM_EPS = 0.00001
MASKED = -1e30

SEQS = 64
MODEL = 4096
HEAD = 128
KVL = 4
GROUP = 4
HEADS = KVL * GROUP
SLOTS = 128
ROWS = SLOTS * KVL
QKV_N = (GROUP + 2) * HEAD
UP_N = 512
UP_STEPS = 7
DOWN_K = 3584
HALF_K = DOWN_K // 2
PIECE = 256
CHUNK = 8
VMEM_LIMIT = 63 * 1024 * 1024

F32 = jnp.float32
BF16 = jnp.bfloat16
MESH = pl.DeviceIdType.MESH
VM = pl.BlockSpec(memory_space=pltpu.VMEM)
SM = pl.BlockSpec(memory_space=pltpu.SMEM)
ANY = pl.BlockSpec(memory_space=pl.ANY)


def dot(a, b):
    return jnp.dot(a, b, preferred_element_type=F32)


def place():
    sp = lax.axis_index('sp')
    return lax.axis_index('tp'), sp, sp // 2, lax.rem(sp, 2)


def enter(peers):
    barrier = pltpu.get_barrier_semaphore()
    for peer in peers:
        pl.semaphore_signal(barrier, inc=1, device_id=peer, device_id_type=MESH)
    pl.semaphore_wait(barrier, len(peers))


def remote(src, dst, send, recv, peer):
    return pltpu.make_async_remote_copy(src_ref=src, dst_ref=dst, send_sem=send, recv_sem=recv, device_id=peer, device_id_type=MESH)


def norm_into(pieces, gain, shift, out_ref):
    width = pieces[0]().shape[1]
    total = sum(jnp.sum(p(), axis=1, keepdims=True) for p in pieces)
    mean = total * (1.0 / MODEL)
    square = sum(jnp.sum(jnp.square(p() - mean), axis=1, keepdims=True) for p in pieces)
    scale = lax.rsqrt(square * (1.0 / MODEL) + NORM_EPS)
    for i, p in enumerate(pieces):
        cols = slice(i * width, (i + 1) * width)
        out_ref[:, cols] = ((p() - mean) * scale * gain(cols) + shift(cols)).astype(BF16)


def qkv_kernel(layer, h_ref, cos_ref, sin_ref, gain_ref, shift_ref, bias_ref, w_ref, out_ref, wbuf, u, heads, wsem, ssem, rsem):
    tp, sp, x, c = place()
    loads = []
    for j in range(2):
        cols = pl.ds(pl.multiple_of(c * (2 * QKV_N) + j * QKV_N, 128), QKV_N)
        loads.append(pltpu.make_async_copy(w_ref.at[layer, :, cols], wbuf.at[j], wsem.at[j]))
        loads[-1].start()
    partner = {'sp': sp + 1 - 2 * c}
    norm_into(
        [lambda i=i: h_ref[:, i * 512:(i + 1) * 512].astype(F32) for i in range(8)],
        lambda cols: gain_ref[layer, 0:1, cols].astype(F32),
        lambda cols: shift_ref[layer, 0:1, cols].astype(F32),
        u,
    )
    enter([partner])
    sent = []
    for j in range(2):
        loads[j].wait()
        kv = 2 * c + j
        cols = pl.ds(pl.multiple_of(kv * QKV_N, 128), QKV_N)
        proj = dot(u[...], wbuf[j]) + bias_ref[layer:layer + 1, cols].astype(F32)
        for i in range(GROUP + 2):
            part = proj[:, i * HEAD:(i + 1) * HEAD]
            if i <= GROUP:
                part = part * cos_ref[...] + pltpu.roll(part, HEAD // 2, 1) * sin_ref[...]
            slot = kv * GROUP + i if i < GROUP else HEADS + (i - GROUP) * KVL + kv
            heads[slot] = part.astype(BF16).astype(F32)
        for n, piece in enumerate((pl.ds(kv * GROUP, GROUP), pl.ds(HEADS + kv, 1), pl.ds(HEADS + KVL + kv, 1))):
            copy = remote(heads.at[piece], heads.at[piece], ssem.at[3 * j + n], rsem.at[3 * j + n], partner)
            copy.start()
            sent.append(copy)
    for copy in sent:
        copy.wait()
    out_ref[...] = heads[...]


def project(layer, h, cos, sin, gain, shift, bias, w):
    return pl.pallas_call(
        functools.partial(qkv_kernel, layer),
        out_shape=jax.ShapeDtypeStruct((HEADS + 2 * KVL, SEQS, HEAD), F32),
        in_specs=[VM] * 6 + [ANY],
        out_specs=VM,
        scratch_shapes=[
            pltpu.VMEM((2, MODEL, QKV_N), BF16),
            pltpu.VMEM((SEQS, MODEL), BF16),
            pltpu.VMEM((HEADS + 2 * KVL, SEQS, HEAD), F32),
            pltpu.SemaphoreType.DMA((2,)),
            pltpu.SemaphoreType.DMA((6,)),
            pltpu.SemaphoreType.DMA((6,)),
        ],
        compiler_params=pltpu.CompilerParams(collective_id=layer, has_side_effects=True, vmem_limit_bytes=VMEM_LIMIT),
        name=f'qkv_{layer}',
    )(h, cos, sin, gain, shift, bias, w)


def attend_kernel(layer, sparse, pos_ref, heads_ref, kc_ref, vc_ref, *rest):
    if layer:
        rest = rest[2:]
    ko_ref, vo_ref, o_ref, ml_ref, kb, vb, mref, lref, slot_of, keep_of, lsem, ssem = rest
    tp, sp, x, c = place()
    steps = SEQS // CHUNK

    def load(i, n):
        src, buf = ((kc_ref, kb), (vc_ref, vb))[n]
        rows = pl.ds(i * CHUNK, CHUNK)
        return pltpu.make_async_copy(src.at[layer, rows], buf.at[rows], lsem.at[n, i])

    def save(i, n):
        dst, buf = ((ko_ref, kb), (vo_ref, vb))[n]
        rows = pl.ds(i * CHUNK, CHUNK)
        return pltpu.make_async_copy(buf.at[rows], dst.at[layer, rows], ssem.at[n, i])

    for i in range(steps):
        for n in range(2):
            load(i, n).start()
    row = lax.broadcasted_iota(jnp.int32, (HEADS, ROWS), 0)
    col = lax.broadcasted_iota(jnp.int32, (HEADS, ROWS), 1)
    slot = sp * SLOTS + col // KVL
    slot_of[...] = jnp.where(lax.rem(col, KVL) == row // GROUP, slot, jnp.int32(1 << 30))
    if sparse:
        block = slot // BLOCK_SIZE
        vertical = lax.rem(block + tp * HEADS + row + 1, VERT_STRIDE) == 0
        keep_of[...] = jnp.where(vertical, jnp.int32(1 << 20), block)
    mref[...] = jnp.zeros_like(mref)
    lref[...] = jnp.ones_like(lref)
    lane = lax.broadcasted_iota(jnp.int32, (HEADS, HEAD), 1)
    row16 = lax.broadcasted_iota(jnp.int32, (4 * KVL, HEAD), 0)

    def body(i, _):
        for n in range(2):
            load(i, n).wait()
        for s in range(CHUNK):
            b = i * CHUNK + s
            t = pos_ref[b] - sp * SLOTS
            inside = jnp.logical_and(t >= 0, t < SLOTS)
            t = jnp.clip(t, 0, SLOTS - 1)
            base = pl.multiple_of((t // 4) * (4 * KVL), 4 * KVL)
            hit = jnp.logical_and(row16 // KVL == lax.rem(t, 4), inside)
            new = heads_ref[pl.ds(HEADS * SEQS + b, 2 * KVL, stride=SEQS), :]
            for buf, part in ((kb, new[:KVL]), (vb, new[KVL:])):
                tile = buf[b, pl.ds(base, 4 * KVL), :].astype(F32)
                buf[b, pl.ds(base, 4 * KVL), :] = jnp.where(hit, jnp.concatenate([part] * 4, axis=0), tile).astype(BF16)
        for n in range(2):
            save(i, n).start()
        for first in range(0, CHUNK, 4):
            ids = [i * CHUNK + first + s for s in range(4)]
            keeps, scores = [], []
            for b in ids:
                q = heads_ref[pl.ds(b, HEADS, stride=SEQS), :].astype(BF16)
                raw = lax.dot_general(q, kb[b], (((1,), (1,)), ((), ())), preferred_element_type=F32)
                pos = pos_ref[b]
                keep = slot_of[...] <= pos
                if sparse:
                    keep = jnp.logical_and(keep, pos // BLOCK_SIZE - keep_of[...] < LOCAL_BLOCKS)
                keeps.append(keep)
                scores.append(jnp.where(keep, raw * (1.0 / HEAD), MASKED))
            weights = []
            for b, keep, score in zip(ids, keeps, scores):
                peak = jnp.max(score, axis=1, keepdims=True)
                weight = jnp.where(keep, jnp.exp(score - peak), 0.0)
                weights.append(weight.astype(BF16))
                mref[...] = jnp.where(lane == b, peak, mref[...])
                lref[...] = jnp.where(lane == b, jnp.sum(weight, axis=1, keepdims=True), lref[...])
            for b, weight in zip(ids, weights):
                o_ref[pl.ds(b, HEADS, stride=SEQS), :] = dot(weight, vb[b])
        return 0

    lax.fori_loop(0, steps, body, 0)
    for kv in range(KVL):
        ml_ref[kv, 0:GROUP] = mref[kv * GROUP:(kv + 1) * GROUP]
        ml_ref[kv, GROUP:2 * GROUP] = lref[kv * GROUP:(kv + 1) * GROUP]
    for i in range(steps):
        for n in range(2):
            save(i, n).wait()


def attend(layer, positions, heads, kc, vc, *done):
    cache = jax.ShapeDtypeStruct(kc.shape, BF16)
    return pl.pallas_call(
        functools.partial(attend_kernel, layer, layer == 0),
        out_shape=(cache, cache, jax.ShapeDtypeStruct((HEADS * SEQS, HEAD), F32), jax.ShapeDtypeStruct((KVL, 2 * GROUP, HEAD), F32)),
        in_specs=[SM, VM, ANY, ANY] + [ANY] * len(done),
        out_specs=(ANY, ANY, VM, VM),
        scratch_shapes=[
            pltpu.VMEM((SEQS, ROWS, HEAD), BF16),
            pltpu.VMEM((SEQS, ROWS, HEAD), BF16),
            pltpu.VMEM((HEADS, HEAD), F32),
            pltpu.VMEM((HEADS, HEAD), F32),
            pltpu.VMEM((HEADS, ROWS), jnp.int32),
            pltpu.VMEM((HEADS, ROWS), jnp.int32),
            pltpu.SemaphoreType.DMA((2, SEQS // CHUNK)),
            pltpu.SemaphoreType.DMA((2, SEQS // CHUNK)),
        ],
        input_output_aliases={4: 0, 5: 1} if done else {},
        compiler_params=pltpu.CompilerParams(vmem_limit_bytes=VMEM_LIMIT),
        name=f'attend_{layer}',
    )(positions, heads, kc, vc, *done)


def mlp_kernel(
    layer, o_ref, ml_ref, h_ref, gain_ref, shift_ref, bd_ref, bu_ref, bn_ref, wd_ref, wu_ref, wn_ref, out_ref,
    wd, wu, wn, mls, fromcore, tosend, kept, fromx, mine, other, ob, part, ra, rb, xs, u, mf, mp, mb,
    wsem, mls_s, mls_r, o_s, o_r, m_s, m_r, c_s, c_r,
):
    tp, sp, x, c = place()
    y = tp
    core_peer = {'sp': sp + 1 - 2 * c}
    x_peer = {'sp': lax.rem(sp + 2, 4)}
    x_diag = {'sp': 2 * (1 - x) + 1 - c}
    y_peer = {'tp': 1 - tp}
    quarter = [2 * (1 - x) + 1 - y, 2 * (1 - x) + y, 2 * x + 1 - y, 2 * x + y]

    def cols_of(k):
        return pl.ds(pl.multiple_of(c * 2048 + quarter[k] * 512, 512), 512)

    def load_dense(k):
        return pltpu.make_async_copy(wd_ref.at[layer, pl.ds(pl.multiple_of(x * 1024, 1024), 1024), cols_of(k)], wd.at[k], wsem.at[k])

    def load_up(j):
        cols = pl.ds(pl.multiple_of(x * 7168 + c * 3584 + j * UP_N, UP_N), UP_N)
        return pltpu.make_async_copy(wu_ref.at[layer, :, cols], wu.at[j], wsem.at[4 + j])

    def load_down(k):
        return pltpu.make_async_copy(wn_ref.at[layer, pl.ds(pl.multiple_of(x * DOWN_K, DOWN_K), DOWN_K), cols_of(k)], wn.at[k], wsem.at[4 + UP_STEPS + k])

    for k in range(4):
        load_dense(k).start()
    for j in range(UP_STEPS):
        load_up(j).start()
    for k in range(4):
        load_down(k).start()
    enter([core_peer, x_peer, x_diag, y_peer])

    waits = []

    def send(*args):
        copy = remote(*args)
        copy.start()
        waits.append(copy)
        return copy

    stats = []
    for r in range(1, 4):
        stats.append(send(ml_ref, mls.at[sp], mls_s.at[r - 1], mls_r.at[r - 1], {'sp': lax.rem(sp + r, 4)}))
    slabs = [None, None]
    for n, xd in enumerate((1 - x, x)):
        src = o_ref.at[pl.ds((2 * xd + 1 - c) * GROUP, GROUP)]
        slabs[n] = send(src, fromcore.at[n], o_s.at[n], o_r.at[n], core_peer)
    mls[sp] = ml_ref[...]
    for copy in stats:
        copy.wait_recv()
    rows = []
    for xd in (1 - x, x):
        kv = 2 * xd + c
        tiles = [mls[i, kv] for i in range(4)]
        top = functools.reduce(jnp.maximum, [t[:GROUP] for t in tiles])
        norm = sum(jnp.exp(t[:GROUP] - top) * t[GROUP:] for t in tiles)
        for who in (sp, sp + 1 - 2 * c):
            rows.append(jnp.exp(mls[who, kv][:GROUP] - top) / norm)
    scale = jnp.concatenate(rows + [jnp.zeros((HEAD - 4 * GROUP, HEAD), F32)], axis=0).T[:SEQS]
    for n, (xd, out) in enumerate(((1 - x, tosend), (x, kept))):
        slabs[n].wait_recv()
        kv = 2 * xd + c
        for g in range(GROUP):
            i = 2 * n * GROUP + g
            out[g] = o_ref[kv * GROUP + g] * scale[:, i:i + 1] + fromcore[n, g] * scale[:, i + GROUP:i + GROUP + 1]
        if n == 0:
            cross = send(tosend, fromx, o_s.at[2], o_r.at[2], x_peer)
    cross.wait_recv()
    for g in range(GROUP):
        val = (kept[g] + fromx[g]).astype(BF16)
        mine[g] = val.astype(F32)
        ob[:, pl.ds(pl.multiple_of(c * 512 + g * HEAD, HEAD), HEAD)] = val
    share = send(mine, other, o_s.at[3], o_r.at[3], core_peer)
    share.wait_recv()
    for g in range(GROUP):
        ob[:, pl.ds(pl.multiple_of((1 - c) * 512 + g * HEAD, HEAD), HEAD)] = other[g].astype(BF16)

    own = (c * 4 + quarter[3]) * 2

    def all_reduce(ph, chunk, residual, bias_ref):
        def post(i, src, dst, peer):
            return send(src, dst, c_s.at[ph, i], c_r.at[ph, i], peer)

        def keep(k):
            val = chunk(k)
            part[ph, k, 0] = val[:, :PIECE]
            part[ph, k, 1] = val[:, PIECE:]

        keep(0)
        a0 = post(0, part.at[ph, 0, 0], ra.at[ph, 0], x_peer)
        b0 = post(1, part.at[ph, 0, 1], rb.at[ph, 0], y_peer)
        keep(1)
        a1 = post(2, part.at[ph, 1, 0], ra.at[ph, 1], x_peer)
        keep(2)
        b1 = post(3, part.at[ph, 2, 1], rb.at[ph, 1], y_peer)
        keep(3)
        b0.wait_recv()
        part[ph, 1, 1] = part[ph, 1, 1] + rb[ph, 0]
        b2 = post(4, part.at[ph, 1, 1], rb.at[ph, 2], x_peer)
        a0.wait_recv()
        part[ph, 2, 0] = part[ph, 2, 0] + ra[ph, 0]
        a2 = post(5, part.at[ph, 2, 0], ra.at[ph, 2], y_peer)
        gather = {}
        for half, (first, second, landed) in enumerate(((a1, a2, ra), (b1, b2, rb))):
            first.wait_recv()
            second.wait_recv()
            cols = pl.ds(pl.multiple_of((own + half) * PIECE, PIECE), PIECE)
            full = part[ph, 3, half] + landed[ph, 1] + landed[ph, 2]
            xs[ph, own + half] = (residual(half, cols) + full + bias_ref[layer:layer + 1, cols].astype(F32)).astype(BF16).astype(F32)
            mine_ref = xs.at[ph, own + half]
            for n, peer in enumerate((x_peer, y_peer, core_peer) if half == 0 else (y_peer, x_peer, core_peer)):
                gather[half, n] = post(6 + 3 * half + n, mine_ref, mine_ref, peer)
        base = c * 8
        from_x = base + quarter[1] * 2
        from_y = base + quarter[2] * 2
        far = base + quarter[0] * 2

        def forward(i, piece, peer):
            ref = xs.at[ph, piece]
            return post(i, ref, ref, peer)

        gather[0, 0].wait_recv()
        far_a = forward(12, from_x, y_peer)
        arrived = [forward(14, from_x, core_peer)]
        gather[1, 0].wait_recv()
        far_b = forward(13, from_y + 1, x_peer)
        arrived.append(forward(15, from_y + 1, core_peer))
        gather[0, 1].wait_recv()
        arrived.append(forward(16, from_y, core_peer))
        gather[1, 1].wait_recv()
        arrived.append(forward(17, from_x + 1, core_peer))
        far_a.wait_recv()
        arrived.append(forward(18, far, core_peer))
        far_b.wait_recv()
        arrived.append(forward(19, far + 1, core_peer))
        for copy in arrived + [gather[0, 2], gather[1, 2]]:
            copy.wait_recv()

    def dense_chunk(k):
        load_dense(k).wait()
        return dot(ob[...], wd[k])

    all_reduce(0, dense_chunk, lambda half, cols: h_ref[:, cols].astype(F32), bd_ref)
    norm_into(
        [lambda i=i: xs[0, i] for i in range(16)],
        lambda cols: gain_ref[layer, 1:2, cols].astype(F32),
        lambda cols: shift_ref[layer, 1:2, cols].astype(F32),
        u,
    )
    take = (lax.broadcasted_iota(jnp.int32, (2 * HEAD, HEAD), 0) == 2 * lax.broadcasted_iota(jnp.int32, (2 * HEAD, HEAD), 1)).astype(BF16)
    even = lax.rem(lax.broadcasted_iota(jnp.int32, (SEQS, UP_N), 1), 2) == 0

    def share_m(j):
        return remote(mf.at[j], mp.at[j], m_s.at[j], m_r.at[j], core_peer)

    def up_step(j, _):
        load_up(j).wait()
        cols = pl.ds(pl.multiple_of(x * 7168 + c * 3584 + j * UP_N, UP_N), UP_N)
        val = dot(u[...], wu[j]) + bu_ref[layer:layer + 1, cols].astype(F32)
        gate = jnp.minimum(val, GELU_LIMIT)
        gate = gate * (1.0 / (1.0 + jnp.exp(-1.702 * gate)))
        linear = jnp.clip(val, -GELU_LIMIT, GELU_LIMIT) + 1.0
        mixed = jnp.where(even, gate * pltpu.roll(linear, UP_N - 1, 1), 0.0).astype(BF16)
        packed = jnp.concatenate([dot(mixed[:, i:i + 2 * HEAD], take) for i in range(0, UP_N, 2 * HEAD)], axis=1)
        mf[j] = packed
        share_m(j).start()
        mb[:, pl.ds(pl.multiple_of(c * HALF_K + j * 256, 256), 256)] = packed.astype(BF16)
        return 0

    lax.fori_loop(0, UP_STEPS, up_step, 0)
    for j in range(UP_STEPS):
        share_m(j).wait()
        mb[:, pl.ds(pl.multiple_of((1 - c) * HALF_K + j * 256, 256), 256)] = mp[j].astype(BF16)

    def down_chunk(k):
        load_down(k).wait()
        return dot(mb[...], wn[k])

    all_reduce(1, down_chunk, lambda half, cols: xs[0, own + half], bn_ref)
    for i in range(16):
        out_ref[:, i * PIECE:(i + 1) * PIECE] = xs[1, i].astype(BF16)
    for copy in waits:
        copy.wait_send()


def finish(layer, o, ml, h, gain, shift, bd, bu, bn, wd, wu, wn):
    slab = pltpu.VMEM((GROUP, SEQS, HEAD), F32)
    dma = pltpu.SemaphoreType.DMA
    return pl.pallas_call(
        functools.partial(mlp_kernel, layer),
        out_shape=jax.ShapeDtypeStruct((SEQS, MODEL), BF16),
        in_specs=[VM] * 8 + [ANY] * 3,
        out_specs=VM,
        scratch_shapes=[
            pltpu.VMEM((4, 1024, 512), BF16),
            pltpu.VMEM((UP_STEPS, MODEL, UP_N), BF16),
            pltpu.VMEM((4, DOWN_K, 512), BF16),
            pltpu.VMEM((4, KVL, 2 * GROUP, HEAD), F32),
            pltpu.VMEM((2, GROUP, SEQS, HEAD), F32),
            slab, slab, slab, slab, slab,
            pltpu.VMEM((SEQS, 1024), BF16),
            pltpu.VMEM((2, 4, 2, SEQS, PIECE), F32),
            pltpu.VMEM((2, 3, SEQS, PIECE), F32),
            pltpu.VMEM((2, 3, SEQS, PIECE), F32),
            pltpu.VMEM((2, 16, SEQS, PIECE), F32),
            pltpu.VMEM((SEQS, MODEL), BF16),
            pltpu.VMEM((UP_STEPS, SEQS, 256), F32),
            pltpu.VMEM((UP_STEPS, SEQS, 256), F32),
            pltpu.VMEM((SEQS, DOWN_K), BF16),
            dma((8 + UP_STEPS,)), dma((3,)), dma((3,)), dma((4,)), dma((4,)), dma((UP_STEPS,)), dma((UP_STEPS,)), dma((2, 20)), dma((2, 20)),
        ],
        compiler_params=pltpu.CompilerParams(collective_id=2 + layer, has_side_effects=True, vmem_limit_bytes=VMEM_LIMIT),
        name=f'mlp_{layer}',
    )(o, ml, h, gain, shift, bd, bu, bn, wd, wu, wn)


def solution(mesh):
    cache_spec = P(None, 'dp', 'sp', 'tp', None)
    in_specs = (P('dp', None), P('dp'), cache_spec, cache_spec, P(), P(), P(None, None, 'tp'), P(None, 'tp'), P(None, 'tp', None), P(), P(None, None, 'tp'), P(None, 'tp'), P(None, 'tp', None), P())
    out_specs = (P('dp', None), cache_spec, cache_spec)

    def device_step(hidden, positions, k_cache, v_cache, ln_gain, ln_bias, w_qkv, b_qkv, w_dense, b_dense, w_up, b_up, w_down, b_down):
        half = HEAD // 2
        inv_freq = ROPE_THETA ** (-jnp.arange(half).astype(F32) * (2.0 / HEAD))
        angles = positions.astype(F32)[:, None] * inv_freq[None, :]
        cos = jnp.cos(angles)
        sin = jnp.sin(angles)
        cos = jnp.concatenate([cos, cos], axis=1)
        sin = jnp.concatenate([-sin, sin], axis=1)
        shape = k_cache.shape
        flat = (2, SEQS, ROWS, HEAD)
        kc = k_cache.reshape(flat)
        vc = v_cache.reshape(flat)
        done = ()
        for layer in range(2):
            heads = project(layer, hidden, cos, sin, ln_gain, ln_bias, b_qkv, w_qkv)
            ko, vo, o, ml = attend(layer, positions, heads.reshape(-1, HEAD), kc, vc, *done)
            done = (ko, vo)
            hidden = finish(layer, o.reshape(HEADS, SEQS, HEAD), ml, hidden, ln_gain, ln_bias, b_dense, b_up, b_down, w_dense, w_up, w_down)
        return hidden, done[0].reshape(shape), done[1].reshape(shape)

    return jax.shard_map(device_step, mesh=mesh, in_specs=in_specs, out_specs=out_specs, check_vma=False)
```

time: 567 us -> 167 us (0.29); the launches traced: 556 us -> 166 us
  matrix products: 176 us -> 0 us
  Pallas kernels: 0 us -> 162 us
  waiting for transfers between devices: 148 us -> 0 us
  other arithmetic: 126 us -> 1.58 us
  local copies, waits for them, and re-layouts: 91 us -> 1.87 us
  between operations: 15.1 us -> 0.69 us
    dot_general x12 -> x0, matrix products: 176 us -> none  [the longest x2 79.2 us: finish_layer(): jnp.dot(normed, w_up, preferred_element_type=jnp.float32)]
    pallas_call x0 -> x6, Pallas kernels: none -> 162 us  [the longest x2 113 us: finish(): pl.pallas_call(functools.partial(mlp_kernel, layer), out_shape=jax.ShapeD...]
    psum x4 -> x0, waiting for transfers between devices: 105 us -> none  [the longest x2 52.9 us: finish_layer(): lax.psum(jnp.dot(gated, w_down, preferred_element_type=jnp.float32), 'tp')]
    select_n x5 -> x0, other arithmetic: 49.4 us -> none  [the longest x3 48.6 us: device_step(): value_rows = jnp.where(hit_mask, v_new[:, None], v_cache[layer_idx])]
    unnamed x32 -> x1, local copies, waits for them, and re-layouts: 45.7 us -> 1.87 us
    all_gather x2 -> x0, waiting for transfers between devices: 42.7 us -> none  [combine_shards(): gathered = lax.all_gather(packed, 'sp')]
    another operation x4 -> x0, other arithmetic: 31 us -> none  [the longest x2 30.3 us: device_step(): return (hidden, jnp.stack(k_layers), jnp.stack(v_layers))]
    slice x10 -> x0, local copies, waits for them, and re-layouts: 25 us -> none  [the longest x2 20.7 us: gegelu(): gate_part = jnp.minimum(col_pairs[..., 0], GELU_LIMIT)]
  transfers between devices with their start and end apart: 6 -> 0, of which waited for: 6 -> 0; matrix products, arithmetic and copies ran while one was open for 10% -> 0% of each run, Pallas kernels for 0% -> 0%
where the time goes in v1:
time: 167 us; the launch traced here: 166 us
  Pallas kernels  162 us (97%)
  local copies, waits for them, and re-layouts  1.87 us (1%)
    pallas_call x2, Pallas kernels, finish(): pl.pallas_call(functools.partial(mlp_kernel, layer), out_shape=jax.ShapeD...  113 us
    pallas_call x2, Pallas kernels, attend(): pl.pallas_call(functools.partial(attend_kernel, layer, layer == 0), out_s...  28.8 us
    pallas_call x2, Pallas kernels, project(): pl.pallas_call(functools.partial(qkv_kernel, layer), out_shape=jax.ShapeD...  19.8 us

profile of v1, /device:TPU:0, one launch (start us, length us, event | category | flops | bytes accessed | tf_op | source)
XLA Modules:
  0.0 166.2 jit_solution(1504326266394140853)
XLA Ops:
  0.6 0.7 convert_element_type.10
  1.3 0.2 fusion
  1.5 0.7 pad_maximum_fusion
  2.2 10.1 %qkv_0.1 = f32[24,64,128]{2,1,0:T(8,128)} custom-call(bf16[64,4096]{1,0:T(8,128)(2,1)} %h_ref.3, f32[64,128]{1,0:T(8,128)} %get-tuple-element.22.cos_ref, f32[64,128]{1,0:T(8,128)} %get-tuple-element.23.sin_ref, bf16[2,2,4096]{2,1,0:T(2,128)(2,1)} %gain_ref.7, bf16[2,2,4096]{2,1,0:T(2,128)(2,1)} %shift_ref.7, bf16[2,3072]{1,0:T(2,128)(2,1)} %bias_ref.3, ...), custom_call_target="tpu_custom_call" | custom-call | tf_op jit(solution)/shard_map/qkv_0/pallas_call | solution.py:111
  12.3 14.4 %attend_0.1 = (bf16[2,64,512,128]{3,2,1,0:T(8,128)(2,1)}, bf16[2,64,512,128]{3,2,1,0:T(8,128)(2,1)}, f32[1024,128]{1,0:T(8,128)}, f32[4,8,128]{2,1,0:T(8,128)}) custom-call(s32[64]{0:T(128)} %pos_ref.3, f32[1536,128]{1,0:T(8,128)} %bitcast.15, bf16[2,64,512,128]{3,2,1,0:T(8,128)(2,1)} %bitcast.8, bf16[2,64,512,128]{3,2,1,0:T(8,128)(2,1)} %bitcast.10), custom_call_target="tpu_custom_call" | custom-call | tf_op jit(solution)/shard_map/attend_0/pallas_call | solution.py:212
  26.7 57.1 %mlp_0.1.h_ref = bf16[64,4096]{1,0:T(8,128)(2,1)} custom-call(f32[16,64,128]{2,1,0:T(8,128)} %bitcast.17, f32[4,8,128]{2,1,0:T(8,128)} %get-tuple-element.12.ml_ref, bf16[64,4096]{1,0:T(8,128)(2,1)} %h_ref.3, bf16[2,2,4096]{2,1,0:T(2,128)(2,1)} %gain_ref.7, bf16[2,2,4096]{2,1,0:T(2,128)(2,1)} %shift_ref.7, bf16[2,4096]{1,0:T(2,128)(2,1)} %bd_ref.3, ...), custom_call_target="tpu_custom_call" | custom-call | tf_op jit(solution)/shard_map/mlp_0/pallas_call | solution.py:423
  83.8 9.7 %qkv_1.1 = f32[24,64,128]{2,1,0:T(8,128)} custom-call(bf16[64,4096]{1,0:T(8,128)(2,1)} %mlp_0.1.h_ref, f32[64,128]{1,0:T(8,128)} %get-tuple-element.22.cos_ref, f32[64,128]{1,0:T(8,128)} %get-tuple-element.23.sin_ref, bf16[2,2,4096]{2,1,0:T(2,128)(2,1)} %gain_ref.7, bf16[2,2,4096]{2,1,0:T(2,128)(2,1)} %shift_ref.7, bf16[2,3072]{1,0:T(2,128)(2,1)} %bias_ref.3, ...), custom_call_target="tpu_custom_call" | custom-call | tf_op jit(solution)/shard_map/qkv_1/pallas_call | solution.py:111
  93.6 14.4 %attend_1.1 = (bf16[2,64,512,128]{3,2,1,0:T(8,128)(2,1)}, bf16[2,64,512,128]{3,2,1,0:T(8,128)(2,1)}, f32[1024,128]{1,0:T(8,128)}, f32[4,8,128]{2,1,0:T(8,128)}) custom-call(s32[64]{0:T(128)} %pos_ref.3, f32[1536,128]{1,0:T(8,128)} %bitcast.14, bf16[2,64,512,128]{3,2,1,0:T(8,128)(2,1)} %bitcast.9, ...), custom_call_target="tpu_custom_call", output_to_operand_aliasing={{0}: (4, {}), {1}: (5, {})} | custom-call | tf_op jit(solution)/shard_map/attend_1/pallas_call | solution.py:212
  108.0 56.4 %mlp_1.1 = bf16[64,4096]{1,0:T(8,128)(2,1)} custom-call(f32[16,64,128]{2,1,0:T(8,128)} %bitcast.16, f32[4,8,128]{2,1,0:T(8,128)} %get-tuple-element.16.ml_ref, bf16[64,4096]{1,0:T(8,128)(2,1)} %mlp_0.1.h_ref, bf16[2,2,4096]{2,1,0:T(2,128)(2,1)} %gain_ref.7, bf16[2,2,4096]{2,1,0:T(2,128)(2,1)} %shift_ref.7, bf16[2,4096]{1,0:T(2,128)(2,1)} %bd_ref.3, ...), custom_call_target="tpu_custom_call" | custom-call | tf_op jit(solution)/shard_map/mlp_1/pallas_call | solution.py:423
  164.4 1.9 %copy.22 = bf16[64,4096]{1,0:T(8,128)(2,1)} copy(bf16[64,4096]{1,0:T(8,128)(2,1)} %mlp_1.1) | data formatting | bytes 1048576
  (1 shorter events, 0.0 us)

commit v2 on v1

--- a/solution.py
+++ b/solution.py
@@ -2,6 +2,7 @@
 
 import jax
 import jax.numpy as jnp
+import numpy as np
 from jax import lax
 from jax.experimental import pallas as pl
 from jax.experimental.pallas import tpu as pltpu
@@ -30,7 +31,7 @@
 HALF_K = DOWN_K // 2
 PIECE = 256
 CHUNK = 8
-VMEM_LIMIT = 63 * 1024 * 1024
+MIB = 1024 * 1024
 
 F32 = jnp.float32
 BF16 = jnp.bfloat16
@@ -71,13 +72,53 @@
         out_ref[:, cols] = ((p() - mean) * scale * gain(cols) + shift(cols)).astype(BF16)
 
 
-def qkv_kernel(layer, h_ref, cos_ref, sin_ref, gain_ref, shift_ref, bias_ref, w_ref, out_ref, wbuf, u, heads, wsem, ssem, rsem):
+def rope_tables(pos_ref, freq_ref, cos_ref, sin_ref):
+    row = lax.broadcasted_iota(jnp.int32, (8, HEAD), 0)
+    sign = jnp.where(lax.broadcasted_iota(jnp.int32, (8, HEAD), 1) < HEAD // 2, -1.0, 1.0)
+    for first in range(0, SEQS, 8):
+        pos = jnp.zeros((8, HEAD), jnp.int32)
+        for i in range(8):
+            pos = jnp.where(row == i, pos_ref[first + i], pos)
+        angle = pos.astype(F32) * freq_ref[...]
+        cos_ref[first:first + 8] = jnp.cos(angle)
+        sin_ref[first:first + 8] = jnp.sin(angle) * sign
+
+
+def load_qkv(layer, c, w_ref, wbuf, sem):
+    loads = []
+    for j in range(3):
+        cols = pl.ds(pl.multiple_of(c * (2 * QKV_N) + j * UP_N, UP_N), UP_N)
+        loads.append(pltpu.make_async_copy(w_ref.at[layer, :, cols], wbuf.at[j], sem.at[j]))
+        loads[-1].start()
+    return loads
+
+
+def qkv_phase(layer, c, partner, u, wbuf, loads, bias_ref, cos_ref, sin_ref, heads, ssem, rsem):
+    sent = []
+    for j in range(3):
+        loads[j].wait()
+        cols = pl.ds(pl.multiple_of(c * (2 * QKV_N) + j * UP_N, UP_N), UP_N)
+        proj = dot(u[...], wbuf[j]) + bias_ref[layer:layer + 1, cols].astype(F32)
+        for n in range(4):
+            local, i = divmod(4 * j + n, GROUP + 2)
+            kv = 2 * c + local
+            part = proj[:, n * HEAD:(n + 1) * HEAD]
+            if i <= GROUP:
+                part = part * cos_ref[...] + pltpu.roll(part, HEAD // 2, 1) * sin_ref[...]
+            slot = kv * GROUP + i if i < GROUP else HEADS + (i - GROUP) * KVL + kv
+            heads[slot] = part.astype(BF16).astype(F32)
+            piece = {GROUP - 1: pl.ds(kv * GROUP, GROUP), GROUP: pl.ds(HEADS + kv, 1), GROUP + 1: pl.ds(HEADS + KVL + kv, 1)}.get(i)
+            if piece is not None:
+                k = len(sent)
+                sent.append(remote(heads.at[piece], heads.at[piece], ssem.at[k], rsem.at[k], partner))
+                sent[-1].start()
+    for copy in sent:
+        copy.wait()
+
+
+def qkv_kernel(layer, pos_ref, freq_ref, h_ref, gain_ref, shift_ref, bias_ref, w_ref, out_ref, wbuf, u, heads, cos, sin, wsem, ssem, rsem):
     tp, sp, x, c = place()
-    loads = []
-    for j in range(2):
-        cols = pl.ds(pl.multiple_of(c * (2 * QKV_N) + j * QKV_N, 128), QKV_N)
-        loads.append(pltpu.make_async_copy(w_ref.at[layer, :, cols], wbuf.at[j], wsem.at[j]))
-        loads[-1].start()
+    loads = load_qkv(layer, c, w_ref, wbuf, wsem)
     partner = {'sp': sp + 1 - 2 * c}
     norm_into(
         [lambda i=i: h_ref[:, i * 512:(i + 1) * 512].astype(F32) for i in range(8)],
@@ -85,45 +126,34 @@
         lambda cols: shift_ref[layer, 0:1, cols].astype(F32),
         u,
     )
+    rope_tables(pos_ref, freq_ref, cos, sin)
     enter([partner])
-    sent = []
-    for j in range(2):
-        loads[j].wait()
-        kv = 2 * c + j
-        cols = pl.ds(pl.multiple_of(kv * QKV_N, 128), QKV_N)
-        proj = dot(u[...], wbuf[j]) + bias_ref[layer:layer + 1, cols].astype(F32)
-        for i in range(GROUP + 2):
-            part = proj[:, i * HEAD:(i + 1) * HEAD]
-            if i <= GROUP:
-                part = part * cos_ref[...] + pltpu.roll(part, HEAD // 2, 1) * sin_ref[...]
-            slot = kv * GROUP + i if i < GROUP else HEADS + (i - GROUP) * KVL + kv
-            heads[slot] = part.astype(BF16).astype(F32)
-        for n, piece in enumerate((pl.ds(kv * GROUP, GROUP), pl.ds(HEADS + kv, 1), pl.ds(HEADS + KVL + kv, 1))):
-            copy = remote(heads.at[piece], heads.at[piece], ssem.at[3 * j + n], rsem.at[3 * j + n], partner)
-            copy.start()
-            sent.append(copy)
-    for copy in sent:
-        copy.wait()
+    qkv_phase(layer, c, partner, u, wbuf, loads, bias_ref, cos, sin, heads, ssem, rsem)
     out_ref[...] = heads[...]
 
 
-def project(layer, h, cos, sin, gain, shift, bias, w):
+HEADS_SHAPE = (HEADS + 2 * KVL, SEQS, HEAD)
+
+
+def project(layer, positions, freq, h, gain, shift, bias, w):
     return pl.pallas_call(
         functools.partial(qkv_kernel, layer),
-        out_shape=jax.ShapeDtypeStruct((HEADS + 2 * KVL, SEQS, HEAD), F32),
-        in_specs=[VM] * 6 + [ANY],
+        out_shape=jax.ShapeDtypeStruct(HEADS_SHAPE, F32),
+        in_specs=[SM] + [VM] * 5 + [ANY],
         out_specs=VM,
         scratch_shapes=[
-            pltpu.VMEM((2, MODEL, QKV_N), BF16),
+            pltpu.VMEM((3, MODEL, UP_N), BF16),
             pltpu.VMEM((SEQS, MODEL), BF16),
-            pltpu.VMEM((HEADS + 2 * KVL, SEQS, HEAD), F32),
-            pltpu.SemaphoreType.DMA((2,)),
+            pltpu.VMEM(HEADS_SHAPE, F32),
+            pltpu.VMEM((SEQS, HEAD), F32),
+            pltpu.VMEM((SEQS, HEAD), F32),
+            pltpu.SemaphoreType.DMA((3,)),
             pltpu.SemaphoreType.DMA((6,)),
             pltpu.SemaphoreType.DMA((6,)),
         ],
-        compiler_params=pltpu.CompilerParams(collective_id=layer, has_side_effects=True, vmem_limit_bytes=VMEM_LIMIT),
+        compiler_params=pltpu.CompilerParams(collective_id=layer, has_side_effects=True, vmem_limit_bytes=63 * MIB),
         name=f'qkv_{layer}',
-    )(h, cos, sin, gain, shift, bias, w)
+    )(positions, freq, h, gain, shift, bias, w)
 
 
 def attend_kernel(layer, sparse, pos_ref, heads_ref, kc_ref, vc_ref, *rest):
@@ -225,21 +255,26 @@
             pltpu.SemaphoreType.DMA((2, SEQS // CHUNK)),
         ],
         input_output_aliases={4: 0, 5: 1} if done else {},
-        compiler_params=pltpu.CompilerParams(vmem_limit_bytes=VMEM_LIMIT),
+        compiler_params=pltpu.CompilerParams(vmem_limit_bytes=63 * MIB),
         name=f'attend_{layer}',
     )(positions, heads, kc, vc, *done)
 
 
-def mlp_kernel(
-    layer, o_ref, ml_ref, h_ref, gain_ref, shift_ref, bd_ref, bu_ref, bn_ref, wd_ref, wu_ref, wn_ref, out_ref,
-    wd, wu, wn, mls, fromcore, tosend, kept, fromx, mine, other, ob, part, ra, rb, xs, u, mf, mp, mb,
-    wsem, mls_s, mls_r, o_s, o_r, m_s, m_r, c_s, c_r,
-):
+def mlp_kernel(layer, last, o_ref, ml_ref, h_ref, gain_ref, shift_ref, bd_ref, bu_ref, bn_ref, wd_ref, wu_ref, wn_ref, *rest):
+    if not last:
+        pos_ref, freq_ref, bq_ref, wq_ref, out_ref, heads_out = rest[:6]
+        heads, cos, sin, q_s, q_r = rest[-5:]
+        rest = rest[6:-5]
+    else:
+        out_ref, rest = rest[0], rest[1:]
+    (
+        wd, wu, wn, mls, mlx, fromcore, tosend, kept, fromx, mine, other, ob, part, ra, rb, xs, u, mf, mp, mb, ps,
+        wsem, o_s, o_r, m_s, m_r, c_s, c_r,
+    ) = rest
     tp, sp, x, c = place()
     y = tp
     core_peer = {'sp': sp + 1 - 2 * c}
     x_peer = {'sp': lax.rem(sp + 2, 4)}
-    x_diag = {'sp': 2 * (1 - x) + 1 - c}
     y_peer = {'tp': 1 - tp}
     quarter = [2 * (1 - x) + 1 - y, 2 * (1 - x) + y, 2 * x + 1 - y, 2 * x + y]
 
@@ -262,8 +297,7 @@
         load_up(j).start()
     for k in range(4):
         load_down(k).start()
-    enter([core_peer, x_peer, x_diag, y_peer])
-
+    enter([core_peer, x_peer, y_peer])
     waits = []
 
     def send(*args):
@@ -272,25 +306,28 @@
         waits.append(copy)
         return copy
 
-    stats = []
-    for r in range(1, 4):
-        stats.append(send(ml_ref, mls.at[sp], mls_s.at[r - 1], mls_r.at[r - 1], {'sp': lax.rem(sp + r, 4)}))
+    stats = send(ml_ref, mls, o_s.at[4], o_r.at[4], core_peer)
     slabs = [None, None]
     for n, xd in enumerate((1 - x, x)):
         src = o_ref.at[pl.ds((2 * xd + 1 - c) * GROUP, GROUP)]
         slabs[n] = send(src, fromcore.at[n], o_s.at[n], o_r.at[n], core_peer)
-    mls[sp] = ml_ref[...]
-    for copy in stats:
-        copy.wait_recv()
+
+    def columns(rows):
+        return jnp.concatenate(rows + [jnp.zeros((HEAD - GROUP * len(rows), HEAD), F32)], axis=0).T[:SEQS]
+
+    def merge(one, two):
+        top = jnp.maximum(one[:GROUP], two[:GROUP])
+        first, second = jnp.exp(one[:GROUP] - top), jnp.exp(two[:GROUP] - top)
+        return first, second, top, first * one[GROUP:] + second * two[GROUP:]
+
+    stats.wait_recv()
     rows = []
-    for xd in (1 - x, x):
-        kv = 2 * xd + c
-        tiles = [mls[i, kv] for i in range(4)]
-        top = functools.reduce(jnp.maximum, [t[:GROUP] for t in tiles])
-        norm = sum(jnp.exp(t[:GROUP] - top) * t[GROUP:] for t in tiles)
-        for who in (sp, sp + 1 - 2 * c):
-            rows.append(jnp.exp(mls[who, kv][:GROUP] - top) / norm)
-    scale = jnp.concatenate(rows + [jnp.zeros((HEAD - 4 * GROUP, HEAD), F32)], axis=0).T[:SEQS]
+    for n, xd in enumerate((1 - x, x)):
+        first, second, top, total = merge(ml_ref[2 * xd + c], mls[2 * xd + c])
+        rows += [first, second]
+        mlx[n] = jnp.concatenate([top, total], axis=0)
+    cross_ml = send(mlx.at[0], mlx.at[2], o_s.at[5], o_r.at[5], x_peer)
+    scale = columns(rows)
     for n, (xd, out) in enumerate(((1 - x, tosend), (x, kept))):
         slabs[n].wait_recv()
         kv = 2 * xd + c
@@ -299,9 +336,12 @@
             out[g] = o_ref[kv * GROUP + g] * scale[:, i:i + 1] + fromcore[n, g] * scale[:, i + GROUP:i + GROUP + 1]
         if n == 0:
             cross = send(tosend, fromx, o_s.at[2], o_r.at[2], x_peer)
+    cross_ml.wait_recv()
+    first, second, _, total = merge(mlx[1], mlx[2])
+    scale = columns([first / total, second / total])
     cross.wait_recv()
     for g in range(GROUP):
-        val = (kept[g] + fromx[g]).astype(BF16)
+        val = (kept[g] * scale[:, g:g + 1] + fromx[g] * scale[:, g + GROUP:g + GROUP + 1]).astype(BF16)
         mine[g] = val.astype(F32)
         ob[:, pl.ds(pl.multiple_of(c * 512 + g * HEAD, HEAD), HEAD)] = val
     share = send(mine, other, o_s.at[3], o_r.at[3], core_peer)
@@ -334,15 +374,17 @@
         a0.wait_recv()
         part[ph, 2, 0] = part[ph, 2, 0] + ra[ph, 0]
         a2 = post(5, part.at[ph, 2, 0], ra.at[ph, 2], y_peer)
-        gather = {}
         for half, (first, second, landed) in enumerate(((a1, a2, ra), (b1, b2, rb))):
             first.wait_recv()
             second.wait_recv()
             cols = pl.ds(pl.multiple_of((own + half) * PIECE, PIECE), PIECE)
             full = part[ph, 3, half] + landed[ph, 1] + landed[ph, 2]
             xs[ph, own + half] = (residual(half, cols) + full + bias_ref[layer:layer + 1, cols].astype(F32)).astype(BF16).astype(F32)
-            mine_ref = xs.at[ph, own + half]
-            for n, peer in enumerate((x_peer, y_peer, core_peer) if half == 0 else (y_peer, x_peer, core_peer)):
+        gather = {}
+        for n in range(3):
+            for half in range(2):
+                peer = core_peer if n == 2 else (x_peer, y_peer)[(n + half) % 2]
+                mine_ref = xs.at[ph, own + half]
                 gather[half, n] = post(6 + 3 * half + n, mine_ref, mine_ref, peer)
         base = c * 8
         from_x = base + quarter[1] * 2
@@ -402,34 +444,54 @@
         return 0
 
     lax.fori_loop(0, UP_STEPS, up_step, 0)
+    if not last:
+        loads = load_qkv(layer + 1, c, wq_ref, wu, wsem)
+        rope_tables(pos_ref, freq_ref, cos, sin)
+    own_k = pl.ds(pl.multiple_of(c * HALF_K, HALF_K), HALF_K)
+    other_k = pl.ds(pl.multiple_of((1 - c) * HALF_K, HALF_K), HALF_K)
+    for k in range(4):
+        load_down(k).wait()
+        ps[k] = dot(mb[:, own_k], wn[k, own_k])
     for j in range(UP_STEPS):
         share_m(j).wait()
         mb[:, pl.ds(pl.multiple_of((1 - c) * HALF_K + j * 256, 256), 256)] = mp[j].astype(BF16)
 
     def down_chunk(k):
-        load_down(k).wait()
-        return dot(mb[...], wn[k])
+        return ps[k] + dot(mb[:, other_k], wn[k, other_k])
 
     all_reduce(1, down_chunk, lambda half, cols: xs[0, own + half], bn_ref)
     for i in range(16):
         out_ref[:, i * PIECE:(i + 1) * PIECE] = xs[1, i].astype(BF16)
+    if not last:
+        norm_into(
+            [lambda i=i: xs[1, i] for i in range(16)],
+            lambda cols: gain_ref[layer + 1, 0:1, cols].astype(F32),
+            lambda cols: shift_ref[layer + 1, 0:1, cols].astype(F32),
+            u,
+        )
+        qkv_phase(layer + 1, c, core_peer, u, wu, loads, bq_ref, cos, sin, heads, q_s, q_r)
+        heads_out[...] = heads[...]
     for copy in waits:
         copy.wait_send()
 
 
-def finish(layer, o, ml, h, gain, shift, bd, bu, bn, wd, wu, wn):
+def finish(layer, o, ml, h, gain, shift, bd, bu, bn, wd, wu, wn, *following):
     slab = pltpu.VMEM((GROUP, SEQS, HEAD), F32)
     dma = pltpu.SemaphoreType.DMA
+    last = not following
+    hidden = jax.ShapeDtypeStruct((SEQS, MODEL), BF16)
+    table = pltpu.VMEM((SEQS, HEAD), F32)
     return pl.pallas_call(
-        functools.partial(mlp_kernel, layer),
-        out_shape=jax.ShapeDtypeStruct((SEQS, MODEL), BF16),
-        in_specs=[VM] * 8 + [ANY] * 3,
-        out_specs=VM,
+        functools.partial(mlp_kernel, layer, last),
+        out_shape=hidden if last else (hidden, jax.ShapeDtypeStruct(HEADS_SHAPE, F32)),
+        in_specs=[VM] * 8 + [ANY] * 3 + ([] if last else [SM, VM, VM, ANY]),
+        out_specs=VM if last else (VM, VM),
         scratch_shapes=[
             pltpu.VMEM((4, 1024, 512), BF16),
             pltpu.VMEM((UP_STEPS, MODEL, UP_N), BF16),
             pltpu.VMEM((4, DOWN_K, 512), BF16),
-            pltpu.VMEM((4, KVL, 2 * GROUP, HEAD), F32),
+            pltpu.VMEM((KVL, 2 * GROUP, HEAD), F32),
+            pltpu.VMEM((3, 2 * GROUP, HEAD), F32),
             pltpu.VMEM((2, GROUP, SEQS, HEAD), F32),
             slab, slab, slab, slab, slab,
             pltpu.VMEM((SEQS, 1024), BF16),
@@ -441,11 +503,12 @@
             pltpu.VMEM((UP_STEPS, SEQS, 256), F32),
             pltpu.VMEM((UP_STEPS, SEQS, 256), F32),
             pltpu.VMEM((SEQS, DOWN_K), BF16),
-            dma((8 + UP_STEPS,)), dma((3,)), dma((3,)), dma((4,)), dma((4,)), dma((UP_STEPS,)), dma((UP_STEPS,)), dma((2, 20)), dma((2, 20)),
-        ],
-        compiler_params=pltpu.CompilerParams(collective_id=2 + layer, has_side_effects=True, vmem_limit_bytes=VMEM_LIMIT),
+            pltpu.VMEM((4, SEQS, 512), F32),
+            dma((8 + UP_STEPS,)), dma((6,)), dma((6,)), dma((UP_STEPS,)), dma((UP_STEPS,)), dma((2, 20)), dma((2, 20)),
+        ] + ([] if last else [pltpu.VMEM(HEADS_SHAPE, F32), table, table, dma((6,)), dma((6,))]),
+        compiler_params=pltpu.CompilerParams(collective_id=2 + layer, has_side_effects=True, vmem_limit_bytes=63 * MIB),
         name=f'mlp_{layer}',
-    )(o, ml, h, gain, shift, bd, bu, bn, wd, wu, wn)
+    )(o, ml, h, gain, shift, bd, bu, bn, wd, wu, wn, *following)
 
 
 def solution(mesh):
@@ -454,23 +517,20 @@
     out_specs = (P('dp', None), cache_spec, cache_spec)
 
     def device_step(hidden, positions, k_cache, v_cache, ln_gain, ln_bias, w_qkv, b_qkv, w_dense, b_dense, w_up, b_up, w_down, b_down):
-        half = HEAD // 2
-        inv_freq = ROPE_THETA ** (-jnp.arange(half).astype(F32) * (2.0 / HEAD))
-        angles = positions.astype(F32)[:, None] * inv_freq[None, :]
-        cos = jnp.cos(angles)
-        sin = jnp.sin(angles)
-        cos = jnp.concatenate([cos, cos], axis=1)
-        sin = jnp.concatenate([-sin, sin], axis=1)
+        freq = ROPE_THETA ** (-np.arange(HEAD // 2) * (2.0 / HEAD))
+        freq = jnp.asarray(np.tile(freq, 2)[None].astype(np.float32))
         shape = k_cache.shape
         flat = (2, SEQS, ROWS, HEAD)
         kc = k_cache.reshape(flat)
         vc = v_cache.reshape(flat)
         done = ()
+        heads = project(0, positions, freq, hidden, ln_gain, ln_bias, b_qkv, w_qkv)
         for layer in range(2):
-            heads = project(layer, hidden, cos, sin, ln_gain, ln_bias, b_qkv, w_qkv)
             ko, vo, o, ml = attend(layer, positions, heads.reshape(-1, HEAD), kc, vc, *done)
             done = (ko, vo)
-            hidden = finish(layer, o.reshape(HEADS, SEQS, HEAD), ml, hidden, ln_gain, ln_bias, b_dense, b_up, b_down, w_dense, w_up, w_down)
+            following = () if layer else (positions, freq, b_qkv, w_qkv)
+            out = finish(layer, o.reshape(HEADS, SEQS, HEAD), ml, hidden, ln_gain, ln_bias, b_dense, b_up, b_down, w_dense, w_up, w_down, *following)
+            hidden, heads = out if following else (out, None)
         return hidden, done[0].reshape(shape), done[1].reshape(shape)
 
     return jax.shard_map(device_step, mesh=mesh, in_specs=in_specs, out_specs=out_specs, check_vma=False)

time: 167 us -> 152 us (0.910)
  Pallas kernels: 162 us -> 149 us
    pallas_call x2 -> x1, Pallas kernels: 19.8 us -> 9.55 us  [project(): pl.pallas_call(functools.partial(qkv_kernel, layer), out_shape=jax.ShapeD...]
    pallas_call x2, Pallas kernels: 113 us -> 110 us  [finish(): pl.pallas_call(functools.partial(mlp_kernel, layer, last), out_shape=hidd...]
where the time goes in v2:
time: 152 us; the launch traced here: 151 us
  Pallas kernels  149 us (98%)
  local copies, waits for them, and re-layouts  1.87 us (1%)
    pallas_call x2, Pallas kernels, finish(): pl.pallas_call(functools.partial(mlp_kernel, layer, last), out_shape=hidd...  110 us
    pallas_call x2, Pallas kernels, attend(): pl.pallas_call(functools.partial(attend_kernel, layer, layer == 0), out_s...  28.8 us
    pallas_call x1, Pallas kernels, project(): pl.pallas_call(functools.partial(qkv_kernel, layer), out_shape=jax.ShapeD...  9.55 us

profile of v2, /device:TPU:0, one launch (start us, length us, event | category | flops | bytes accessed | tf_op | source)
XLA Modules:
  0.0 151.3 jit_solution(17242094433767408620)
XLA Ops:
  0.6 9.6 %qkv_0.1 = f32[24,64,128]{2,1,0:T(8,128)} custom-call(s32[64]{0:T(128)} %pos_ref.5, f32[1,128]{1,0:T(1,128)} %constant.2.clone.freq_ref.rest_1_, bf16[64,4096]{1,0:T(8,128)(2,1)} %h_ref.3, bf16[2,2,4096]{2,1,0:T(2,128)(2,1)} %gain_ref.5, bf16[2,2,4096]{2,1,0:T(2,128)(2,1)} %shift_ref.5, bf16[2,3072]{1,0:T(2,128)(2,1)} %rest_2_.1, bf16[2,4096,3072]{2,1,0:T(8,128)(2,1)} %rest_3_.1), custom_call_target="tpu_custom_call" | custom-call | tf_op jit(solution)/shard_map/qkv_0/pallas_call | solution.py:139
  10.2 14.4 %attend_0.1 = (bf16[2,64,512,128]{3,2,1,0:T(8,128)(2,1)}, bf16[2,64,512,128]{3,2,1,0:T(8,128)(2,1)}, f32[1024,128]{1,0:T(8,128)}, f32[4,8,128]{2,1,0:T(8,128)}) custom-call(s32[64]{0:T(128)} %pos_ref.5, f32[1536,128]{1,0:T(8,128)} %bitcast.14, bf16[2,64,512,128]{3,2,1,0:T(8,128)(2,1)} %bitcast.8, bf16[2,64,512,128]{3,2,1,0:T(8,128)(2,1)} %bitcast.10), custom_call_target="tpu_custom_call" | custom-call | tf_op jit(solution)/shard_map/attend_0/pallas_call | solution.py:242
  24.6 59.4 %mlp_0.1 = (bf16[64,4096]{1,0:T(8,128)(2,1)}, f32[24,64,128]{2,1,0:T(8,128)}) custom-call(f32[16,64,128]{2,1,0:T(8,128)} %bitcast.16, f32[4,8,128]{2,1,0:T(8,128)} %get-tuple-element.14.ml_ref, bf16[64,4096]{1,0:T(8,128)(2,1)} %h_ref.3, bf16[2,2,4096]{2,1,0:T(2,128)(2,1)} %gain_ref.5, bf16[2,2,4096]{2,1,0:T(2,128)(2,1)} %shift_ref.5, ...), custom_call_target="tpu_custom_call" | custom-call | tf_op jit(solution)/shard_map/mlp_0/pallas_call | solution.py:484
  84.0 14.4 %attend_1.1 = (bf16[2,64,512,128]{3,2,1,0:T(8,128)(2,1)}, bf16[2,64,512,128]{3,2,1,0:T(8,128)(2,1)}, f32[1024,128]{1,0:T(8,128)}, f32[4,8,128]{2,1,0:T(8,128)}) custom-call(s32[64]{0:T(128)} %pos_ref.5, f32[1536,128]{1,0:T(8,128)} %bitcast.15, bf16[2,64,512,128]{3,2,1,0:T(8,128)(2,1)} %bitcast.9, ...), custom_call_target="tpu_custom_call", output_to_operand_aliasing={{0}: (4, {}), {1}: (5, {})} | custom-call | tf_op jit(solution)/shard_map/attend_1/pallas_call | solution.py:242
  98.5 51.0 %mlp_1.1 = bf16[64,4096]{1,0:T(8,128)(2,1)} custom-call(f32[16,64,128]{2,1,0:T(8,128)} %bitcast.17, f32[4,8,128]{2,1,0:T(8,128)} %get-tuple-element.19.ml_ref, bf16[64,4096]{1,0:T(8,128)(2,1)} %get-tuple-element.20.h_ref, bf16[2,2,4096]{2,1,0:T(2,128)(2,1)} %gain_ref.5, bf16[2,2,4096]{2,1,0:T(2,128)(2,1)} %shift_ref.5, bf16[2,4096]{1,0:T(2,128)(2,1)} %bd_ref.3, ...), custom_call_target="tpu_custom_call" | custom-call | tf_op jit(solution)/shard_map/mlp_1/pallas_call | solution.py:484
  149.4 1.9 %copy.23 = bf16[64,4096]{1,0:T(8,128)(2,1)} copy(bf16[64,4096]{1,0:T(8,128)(2,1)} %mlp_1.1) | data formatting | bytes 1048576

commit v3 on v2

--- a/solution.py
+++ b/solution.py
@@ -32,13 +32,28 @@
 PIECE = 256
 CHUNK = 8
 MIB = 1024 * 1024
+QKV_MIB = 20
+ATTEND_MIB = 8
+MLP_MIB = 40
 
 F32 = jnp.float32
 BF16 = jnp.bfloat16
 MESH = pl.DeviceIdType.MESH
 VM = pl.BlockSpec(memory_space=pltpu.VMEM)
 SM = pl.BlockSpec(memory_space=pltpu.SMEM)
-ANY = pl.BlockSpec(memory_space=pl.ANY)
+HBM = pl.BlockSpec(memory_space=pltpu.HBM)
+
+
+def kept(shape, dtype):
+    return pltpu.VMEM(shape, dtype)
+
+
+def pin(x):
+    return pltpu.with_memory_space_constraint(x, pltpu.HBM)
+
+
+def near(x):
+    return pltpu.with_memory_space_constraint(x, pltpu.VMEM)
 
 
 def dot(a, b):
@@ -84,13 +99,9 @@
         sin_ref[first:first + 8] = jnp.sin(angle) * sign
 
 
-def load_qkv(layer, c, w_ref, wbuf, sem):
-    loads = []
-    for j in range(3):
-        cols = pl.ds(pl.multiple_of(c * (2 * QKV_N) + j * UP_N, UP_N), UP_N)
-        loads.append(pltpu.make_async_copy(w_ref.at[layer, :, cols], wbuf.at[j], sem.at[j]))
-        loads[-1].start()
-    return loads
+def load_qkv(layer, c, w_ref, wbuf, sem, j):
+    cols = pl.ds(pl.multiple_of(c * (2 * QKV_N) + j * UP_N, UP_N), UP_N)
+    return pltpu.make_async_copy(w_ref.at[layer, :, cols], wbuf.at[j], sem.at[j])
 
 
 def qkv_phase(layer, c, partner, u, wbuf, loads, bias_ref, cos_ref, sin_ref, heads, ssem, rsem):
@@ -116,66 +127,107 @@
         copy.wait()
 
 
-def qkv_kernel(layer, pos_ref, freq_ref, h_ref, gain_ref, shift_ref, bias_ref, w_ref, out_ref, wbuf, u, heads, cos, sin, wsem, ssem, rsem):
+def copy_in(pairs, sems):
+    copies = [pltpu.make_async_copy(src, dst, sems.at[i]) for i, (src, dst) in enumerate(pairs)]
+    for copy in copies:
+        copy.start()
+    return copies
+
+
+def cache_copies(layer, kc_ref, vc_ref, k_out, v_out, sems):
+    return [pltpu.make_async_copy(src.at[layer], dst, sems.at[n]) for n, (src, dst) in enumerate(((kc_ref, k_out), (vc_ref, v_out)))]
+
+
+def qkv_kernel(
+    layer, pos_hbm, freq_hbm, h_hbm, gain_hbm, shift_hbm, bias_hbm, w_ref, kc_ref, vc_ref, out_ref, k_out, v_out,
+    wbuf, u, heads, cos, sin, pos, freq, h, gain, shift, bias, isem, wsem, ksem, ssem, rsem,
+):
     tp, sp, x, c = place()
-    loads = load_qkv(layer, c, w_ref, wbuf, wsem)
+    small = copy_in([(h_hbm, h), (gain_hbm, gain), (shift_hbm, shift), (pos_hbm, pos), (freq_hbm, freq), (bias_hbm, bias)], isem)
+    loads = [load_qkv(layer, c, w_ref, wbuf, wsem, j) for j in range(3)]
     partner = {'sp': sp + 1 - 2 * c}
+    for copy in small:
+        copy.wait()
+
+    def begin(j, _):
+        load_qkv(layer, c, w_ref, wbuf, wsem, j).start()
+        return 0
+
+    lax.fori_loop(0, 3, begin, 0)
+    for copy in cache_copies(layer, kc_ref, vc_ref, k_out, v_out, ksem):
+        copy.start()
     norm_into(
-        [lambda i=i: h_ref[:, i * 512:(i + 1) * 512].astype(F32) for i in range(8)],
-        lambda cols: gain_ref[layer, 0:1, cols].astype(F32),
-        lambda cols: shift_ref[layer, 0:1, cols].astype(F32),
+        [lambda i=i: h[:, i * 512:(i + 1) * 512].astype(F32) for i in range(8)],
+        lambda cols: gain[layer, 0:1, cols].astype(F32),
+        lambda cols: shift[layer, 0:1, cols].astype(F32),
         u,
     )
-    rope_tables(pos_ref, freq_ref, cos, sin)
+    rope_tables(pos, freq, cos, sin)
     enter([partner])
-    qkv_phase(layer, c, partner, u, wbuf, loads, bias_ref, cos, sin, heads, ssem, rsem)
+    qkv_phase(layer, c, partner, u, wbuf, loads, bias, cos, sin, heads, ssem, rsem)
     out_ref[...] = heads[...]
+    for copy in cache_copies(layer, kc_ref, vc_ref, k_out, v_out, ksem):
+        copy.wait()
 
 
 HEADS_SHAPE = (HEADS + 2 * KVL, SEQS, HEAD)
 
 
-def project(layer, positions, freq, h, gain, shift, bias, w):
+CACHE = kept((SEQS, ROWS, HEAD), BF16)
+
+
+def project(layer, positions, freq, h, gain, shift, bias, w, kc, vc):
+    dma = pltpu.SemaphoreType.DMA
     return pl.pallas_call(
         functools.partial(qkv_kernel, layer),
-        out_shape=jax.ShapeDtypeStruct(HEADS_SHAPE, F32),
-        in_specs=[SM] + [VM] * 5 + [ANY],
-        out_specs=VM,
+        out_shape=(kept(HEADS_SHAPE, F32), CACHE, CACHE),
+        in_specs=[HBM] * 9,
+        out_specs=(VM, VM, VM),
         scratch_shapes=[
             pltpu.VMEM((3, MODEL, UP_N), BF16),
             pltpu.VMEM((SEQS, MODEL), BF16),
             pltpu.VMEM(HEADS_SHAPE, F32),
             pltpu.VMEM((SEQS, HEAD), F32),
             pltpu.VMEM((SEQS, HEAD), F32),
-            pltpu.SemaphoreType.DMA((3,)),
-            pltpu.SemaphoreType.DMA((6,)),
-            pltpu.SemaphoreType.DMA((6,)),
+            pltpu.SMEM((SEQS,), jnp.int32),
+            pltpu.VMEM((1, HEAD), F32),
+            pltpu.VMEM((SEQS, MODEL), BF16),
+            pltpu.VMEM(gain.shape, BF16),
+            pltpu.VMEM(shift.shape, BF16),
+            pltpu.VMEM(bias.shape, BF16),
+            dma((6,)), dma((3,)), dma((2,)), dma((6,)), dma((6,)),
         ],
-        compiler_params=pltpu.CompilerParams(collective_id=layer, has_side_effects=True, vmem_limit_bytes=63 * MIB),
+        compiler_params=pltpu.CompilerParams(collective_id=layer, has_side_effects=True, vmem_limit_bytes=QKV_MIB * MIB),
         name=f'qkv_{layer}',
-    )(positions, freq, h, gain, shift, bias, w)
-
-
-def attend_kernel(layer, sparse, pos_ref, heads_ref, kc_ref, vc_ref, *rest):
+    )(*map(pin, (positions, freq, h, gain, shift, bias, w, kc, vc)))
+
+
+def attend_kernel(layer, sparse, pos_hbm, heads_ref, kb, vb, *rest):
     if layer:
         rest = rest[2:]
-    ko_ref, vo_ref, o_ref, ml_ref, kb, vb, mref, lref, slot_of, keep_of, lsem, ssem = rest
+    ko_ref, vo_ref, o_ref, ml_ref, pos_ref, mref, lref, slot_of, keep_of, tiles, psem, ssem, tsem = rest
     tp, sp, x, c = place()
     steps = SEQS // CHUNK
-
-    def load(i, n):
-        src, buf = ((kc_ref, kb), (vc_ref, vb))[n]
-        rows = pl.ds(i * CHUNK, CHUNK)
-        return pltpu.make_async_copy(src.at[layer, rows], buf.at[rows], lsem.at[n, i])
+    copy_in([(pos_hbm, pos_ref)], psem)
 
     def save(i, n):
         dst, buf = ((ko_ref, kb), (vo_ref, vb))[n]
         rows = pl.ds(i * CHUNK, CHUNK)
         return pltpu.make_async_copy(buf.at[rows], dst.at[layer, rows], ssem.at[n, i])
 
+    def place_of(b):
+        t = pos_ref[b] - sp * SLOTS
+        inside = jnp.logical_and(t >= 0, t < SLOTS)
+        t = jnp.clip(t, 0, SLOTS - 1)
+        return t, inside, pl.multiple_of((t // 4) * (4 * KVL), 4 * KVL)
+
+    def patch(b, n):
+        base = place_of(b)[2]
+        return pltpu.make_async_copy(tiles.at[n, b], (ko_ref, vo_ref)[n].at[layer, b, pl.ds(base, 4 * KVL)], tsem.at[n])
+
     for i in range(steps):
         for n in range(2):
-            load(i, n).start()
+            save(i, n).start()
     row = lax.broadcasted_iota(jnp.int32, (HEADS, ROWS), 0)
     col = lax.broadcasted_iota(jnp.int32, (HEADS, ROWS), 1)
     slot = sp * SLOTS + col // KVL
@@ -188,87 +240,95 @@
     lref[...] = jnp.ones_like(lref)
     lane = lax.broadcasted_iota(jnp.int32, (HEADS, HEAD), 1)
     row16 = lax.broadcasted_iota(jnp.int32, (4 * KVL, HEAD), 0)
+    copy_of_pos = pltpu.make_async_copy(pos_hbm, pos_ref, psem.at[0])
+    copy_of_pos.wait()
+
+    def repeat(part):
+        return jnp.concatenate([jnp.broadcast_to(part[kv:kv + 1], (GROUP, HEAD)) for kv in range(KVL)], axis=0)
 
     def body(i, _):
-        for n in range(2):
-            load(i, n).wait()
-        for s in range(CHUNK):
-            b = i * CHUNK + s
-            t = pos_ref[b] - sp * SLOTS
-            inside = jnp.logical_and(t >= 0, t < SLOTS)
-            t = jnp.clip(t, 0, SLOTS - 1)
-            base = pl.multiple_of((t // 4) * (4 * KVL), 4 * KVL)
-            hit = jnp.logical_and(row16 // KVL == lax.rem(t, 4), inside)
-            new = heads_ref[pl.ds(HEADS * SEQS + b, 2 * KVL, stride=SEQS), :]
-            for buf, part in ((kb, new[:KVL]), (vb, new[KVL:])):
-                tile = buf[b, pl.ds(base, 4 * KVL), :].astype(F32)
-                buf[b, pl.ds(base, 4 * KVL), :] = jnp.where(hit, jnp.concatenate([part] * 4, axis=0), tile).astype(BF16)
-        for n in range(2):
-            save(i, n).start()
         for first in range(0, CHUNK, 4):
             ids = [i * CHUNK + first + s for s in range(4)]
-            keeps, scores = [], []
+            keeps, hits, scores, news = [], [], [], []
             for b in ids:
-                q = heads_ref[pl.ds(b, HEADS, stride=SEQS), :].astype(BF16)
-                raw = lax.dot_general(q, kb[b], (((1,), (1,)), ((), ())), preferred_element_type=F32)
+                q = heads_ref[pl.ds(b, HEADS, stride=SEQS), :]
+                new = heads_ref[pl.ds(HEADS * SEQS + b, 2 * KVL, stride=SEQS), :]
+                raw = lax.dot_general(q.astype(BF16), kb[b], (((1,), (1,)), ((), ())), preferred_element_type=F32)
                 pos = pos_ref[b]
                 keep = slot_of[...] <= pos
+                hit = slot_of[...] == pos
                 if sparse:
                     keep = jnp.logical_and(keep, pos // BLOCK_SIZE - keep_of[...] < LOCAL_BLOCKS)
+                raw = jnp.where(hit, jnp.sum(q * repeat(new[:KVL]), axis=1, keepdims=True), raw)
                 keeps.append(keep)
+                hits.append(hit)
+                news.append(new)
                 scores.append(jnp.where(keep, raw * (1.0 / HEAD), MASKED))
-            weights = []
-            for b, keep, score in zip(ids, keeps, scores):
+            weights, added = [], []
+            for b, keep, hit, score in zip(ids, keeps, hits, scores):
                 peak = jnp.max(score, axis=1, keepdims=True)
                 weight = jnp.where(keep, jnp.exp(score - peak), 0.0)
-                weights.append(weight.astype(BF16))
                 mref[...] = jnp.where(lane == b, peak, mref[...])
                 lref[...] = jnp.where(lane == b, jnp.sum(weight, axis=1, keepdims=True), lref[...])
-            for b, weight in zip(ids, weights):
-                o_ref[pl.ds(b, HEADS, stride=SEQS), :] = dot(weight, vb[b])
+                weight = weight.astype(BF16).astype(F32)
+                added.append(jnp.sum(jnp.where(hit, weight, 0.0), axis=1, keepdims=True))
+                weights.append(jnp.where(hit, 0.0, weight).astype(BF16))
+            for b, weight, extra, new in zip(ids, weights, added, news):
+                o_ref[pl.ds(b, HEADS, stride=SEQS), :] = dot(weight, vb[b]) + extra * repeat(new[KVL:])
+            for b, new in zip(ids, news):
+                t, inside, base = place_of(b)
+                hit = jnp.logical_and(row16 // KVL == lax.rem(t, 4), inside)
+                for n, buf in enumerate((kb, vb)):
+                    fresh = jnp.concatenate([new[n * KVL:(n + 1) * KVL]] * 4, axis=0)
+                    tiles[n, b] = jnp.where(hit, fresh, buf[b, pl.ds(base, 4 * KVL), :].astype(F32)).astype(BF16)
+        for n in range(2):
+            save(i, n).wait()
+        for s in range(CHUNK):
+            for n in range(2):
+                patch(i * CHUNK + s, n).start()
         return 0
 
     lax.fori_loop(0, steps, body, 0)
     for kv in range(KVL):
         ml_ref[kv, 0:GROUP] = mref[kv * GROUP:(kv + 1) * GROUP]
         ml_ref[kv, GROUP:2 * GROUP] = lref[kv * GROUP:(kv + 1) * GROUP]
-    for i in range(steps):
-        for n in range(2):
-            save(i, n).wait()
-
-
-def attend(layer, positions, heads, kc, vc, *done):
-    cache = jax.ShapeDtypeStruct(kc.shape, BF16)
+
+    for n in range(2):
+        pltpu.make_async_copy(tiles.at[n], (ko_ref, vo_ref)[n].at[layer, :, pl.ds(0, 4 * KVL)], tsem.at[n]).wait()
+
+
+def attend(layer, positions, heads, kb, vb, shape, *done):
+    cache = jax.ShapeDtypeStruct(shape, BF16)
+    dma = pltpu.SemaphoreType.DMA
     return pl.pallas_call(
         functools.partial(attend_kernel, layer, layer == 0),
-        out_shape=(cache, cache, jax.ShapeDtypeStruct((HEADS * SEQS, HEAD), F32), jax.ShapeDtypeStruct((KVL, 2 * GROUP, HEAD), F32)),
-        in_specs=[SM, VM, ANY, ANY] + [ANY] * len(done),
-        out_specs=(ANY, ANY, VM, VM),
+        out_shape=(cache, cache, kept((HEADS * SEQS, HEAD), F32), kept((KVL, 2 * GROUP, HEAD), F32)),
+        in_specs=[HBM, VM, VM, VM] + [HBM] * len(done),
+        out_specs=(HBM, HBM, VM, VM),
         scratch_shapes=[
-            pltpu.VMEM((SEQS, ROWS, HEAD), BF16),
-            pltpu.VMEM((SEQS, ROWS, HEAD), BF16),
+            pltpu.SMEM((SEQS,), jnp.int32),
             pltpu.VMEM((HEADS, HEAD), F32),
             pltpu.VMEM((HEADS, HEAD), F32),
             pltpu.VMEM((HEADS, ROWS), jnp.int32),
             pltpu.VMEM((HEADS, ROWS), jnp.int32),
-            pltpu.SemaphoreType.DMA((2, SEQS // CHUNK)),
-            pltpu.SemaphoreType.DMA((2, SEQS // CHUNK)),
+            pltpu.VMEM((2, SEQS, 4 * KVL, HEAD), BF16),
+            dma((1,)), dma((2, SEQS // CHUNK)), dma((2,)),
         ],
         input_output_aliases={4: 0, 5: 1} if done else {},
-        compiler_params=pltpu.CompilerParams(vmem_limit_bytes=63 * MIB),
+        compiler_params=pltpu.CompilerParams(vmem_limit_bytes=ATTEND_MIB * MIB),
         name=f'attend_{layer}',
-    )(positions, heads, kc, vc, *done)
+    )(pin(positions), *map(near, (heads, kb, vb)), *map(pin, done))
 
 
 def mlp_kernel(layer, last, o_ref, ml_ref, h_ref, gain_ref, shift_ref, bd_ref, bu_ref, bn_ref, wd_ref, wu_ref, wn_ref, *rest):
     if not last:
-        pos_ref, freq_ref, bq_ref, wq_ref, out_ref, heads_out = rest[:6]
-        heads, cos, sin, q_s, q_r = rest[-5:]
-        rest = rest[6:-5]
+        pos_hbm, freq_ref, bq_ref, wq_ref, kc_ref, vc_ref, out_ref, heads_out, k_out, v_out = rest[:10]
+        pos_ref, heads, cos, sin, p_s, k_s, q_s, q_r = rest[-8:]
+        rest = rest[10:-8]
     else:
         out_ref, rest = rest[0], rest[1:]
     (
-        wd, wu, wn, mls, mlx, fromcore, tosend, kept, fromx, mine, other, ob, part, ra, rb, xs, u, mf, mp, mb, ps,
+        wu, mls, mlx, fromcore, tosend, kept, fromx, mine, other, ob, part, ra, rb, xs, u, mf, mp, mb, ps,
         wsem, o_s, o_r, m_s, m_r, c_s, c_r,
     ) = rest
     tp, sp, x, c = place()
@@ -278,25 +338,37 @@
     y_peer = {'tp': 1 - tp}
     quarter = [2 * (1 - x) + 1 - y, 2 * (1 - x) + y, 2 * x + 1 - y, 2 * x + y]
 
+    def turn(k):
+        far, near = 1 - k // 2, k // 2
+        return 2 * (far * (1 - x) + near * x) + (1 - k % 2) * (1 - y) + k % 2 * y
+
     def cols_of(k):
-        return pl.ds(pl.multiple_of(c * 2048 + quarter[k] * 512, 512), 512)
+        return pl.ds(pl.multiple_of(c * 2048 + turn(k) * 512, 512), 512)
 
     def load_dense(k):
-        return pltpu.make_async_copy(wd_ref.at[layer, pl.ds(pl.multiple_of(x * 1024, 1024), 1024), cols_of(k)], wd.at[k], wsem.at[k])
+        return pltpu.make_async_copy(wd_ref.at[layer, pl.ds(pl.multiple_of(x * 1024, 1024), 1024), cols_of(k)], wu.at[UP_STEPS - 1, pl.ds(k * 1024, 1024)], wsem.at[k])
 
     def load_up(j):
         cols = pl.ds(pl.multiple_of(x * 7168 + c * 3584 + j * UP_N, UP_N), UP_N)
         return pltpu.make_async_copy(wu_ref.at[layer, :, cols], wu.at[j], wsem.at[4 + j])
 
     def load_down(k):
-        return pltpu.make_async_copy(wn_ref.at[layer, pl.ds(pl.multiple_of(x * DOWN_K, DOWN_K), DOWN_K), cols_of(k)], wn.at[k], wsem.at[4 + UP_STEPS + k])
+        rows = pl.ds(pl.multiple_of(x * DOWN_K, DOWN_K), DOWN_K)
+        return pltpu.make_async_copy(wn_ref.at[layer, rows, cols_of(k)], wu.at[k, pl.ds(0, DOWN_K)], wsem.at[4 + UP_STEPS + k])
+
+    def load_next(j):
+        return load_qkv(layer + 1, c, wq_ref, wu.at[pl.ds(4, 3)], wsem, j)
 
     for k in range(4):
         load_dense(k).start()
-    for j in range(UP_STEPS):
+    for j in range(UP_STEPS - 1):
         load_up(j).start()
-    for k in range(4):
-        load_down(k).start()
+    if not last:
+        cache = cache_copies(layer + 1, kc_ref, vc_ref, k_out, v_out, k_s)
+        for copy in cache:
+            copy.start()
+        copy_in([(pos_hbm, pos_ref)], p_s)[0].wait()
+        rope_tables(pos_ref, freq_ref, cos, sin)
     enter([core_peer, x_peer, y_peer])
     waits = []
 
@@ -345,15 +417,27 @@
         mine[g] = val.astype(F32)
         ob[:, pl.ds(pl.multiple_of(c * 512 + g * HEAD, HEAD), HEAD)] = val
     share = send(mine, other, o_s.at[3], o_r.at[3], core_peer)
+    own_o = pl.ds(pl.multiple_of(c * 512, 512), 512)
+    other_o = pl.ds(pl.multiple_of((1 - c) * 512, 512), 512)
+
+    def dense_half(k, cols):
+        rows = pl.ds(pl.multiple_of(k * 1024 + cols.start, 512), 512)
+        return dot(ob[:, cols], wu[UP_STEPS - 1, rows])
+
+    for k in range(4):
+        load_dense(k).wait()
+        ps[k] = dense_half(k, own_o)
     share.wait_recv()
     for g in range(GROUP):
         ob[:, pl.ds(pl.multiple_of((1 - c) * 512 + g * HEAD, HEAD), HEAD)] = other[g].astype(BF16)
 
     own = (c * 4 + quarter[3]) * 2
 
-    def all_reduce(ph, chunk, residual, bias_ref):
+    def all_reduce(ph, chunk, residual, bias_ref, after=lambda: None):
         def post(i, src, dst, peer):
-            return send(src, dst, c_s.at[ph, i], c_r.at[ph, i], peer)
+            copy = remote(src, dst, c_s.at[ph, int(i > 5)], c_r.at[ph, i], peer)
+            copy.start()
+            return copy
 
         def keep(k):
             val = chunk(k)
@@ -368,6 +452,7 @@
         keep(2)
         b1 = post(3, part.at[ph, 2, 1], rb.at[ph, 1], y_peer)
         keep(3)
+        after()
         b0.wait_recv()
         part[ph, 1, 1] = part[ph, 1, 1] + rb[ph, 0]
         b2 = post(4, part.at[ph, 1, 1], rb.at[ph, 2], x_peer)
@@ -413,10 +498,9 @@
             copy.wait_recv()
 
     def dense_chunk(k):
-        load_dense(k).wait()
-        return dot(ob[...], wd[k])
-
-    all_reduce(0, dense_chunk, lambda half, cols: h_ref[:, cols].astype(F32), bd_ref)
+        return ps[k] + dense_half(k, other_o)
+
+    all_reduce(0, dense_chunk, lambda half, cols: h_ref[:, cols].astype(F32), bd_ref, load_up(UP_STEPS - 1).start)
     norm_into(
         [lambda i=i: xs[0, i] for i in range(16)],
         lambda cols: gain_ref[layer, 1:2, cols].astype(F32),
@@ -427,7 +511,7 @@
     even = lax.rem(lax.broadcasted_iota(jnp.int32, (SEQS, UP_N), 1), 2) == 0
 
     def share_m(j):
-        return remote(mf.at[j], mp.at[j], m_s.at[j], m_r.at[j], core_peer)
+        return remote(mf.at[j], mp.at[j], m_s.at[0], m_r.at[0], core_peer)
 
     def up_step(j, _):
         load_up(j).wait()
@@ -441,23 +525,30 @@
         mf[j] = packed
         share_m(j).start()
         mb[:, pl.ds(pl.multiple_of(c * HALF_K + j * 256, 256), 256)] = packed.astype(BF16)
+
+        @pl.when(j < 4)
+        def _():
+            load_down(j).start()
+
+        if not last:
+            @pl.when(j >= 4)
+            def _():
+                load_next(j - 4).start()
+
         return 0
 
     lax.fori_loop(0, UP_STEPS, up_step, 0)
-    if not last:
-        loads = load_qkv(layer + 1, c, wq_ref, wu, wsem)
-        rope_tables(pos_ref, freq_ref, cos, sin)
     own_k = pl.ds(pl.multiple_of(c * HALF_K, HALF_K), HALF_K)
     other_k = pl.ds(pl.multiple_of((1 - c) * HALF_K, HALF_K), HALF_K)
     for k in range(4):
         load_down(k).wait()
-        ps[k] = dot(mb[:, own_k], wn[k, own_k])
+        ps[k] = dot(mb[:, own_k], wu[k, own_k])
+    remote(mf, mp, m_s.at[0], m_r.at[0], core_peer).wait()
     for j in range(UP_STEPS):
-        share_m(j).wait()
         mb[:, pl.ds(pl.multiple_of((1 - c) * HALF_K + j * 256, 256), 256)] = mp[j].astype(BF16)
 
     def down_chunk(k):
-        return ps[k] + dot(mb[:, other_k], wn[k, other_k])
+        return ps[k] + dot(mb[:, other_k], wu[k, other_k])
 
     all_reduce(1, down_chunk, lambda half, cols: xs[0, own + half], bn_ref)
     for i in range(16):
@@ -469,8 +560,13 @@
             lambda cols: shift_ref[layer + 1, 0:1, cols].astype(F32),
             u,
         )
-        qkv_phase(layer + 1, c, core_peer, u, wu, loads, bq_ref, cos, sin, heads, q_s, q_r)
+        qkv_phase(layer + 1, c, core_peer, u, wu.at[pl.ds(4, 3)], [load_next(j) for j in range(3)], bq_ref, cos, sin, heads, q_s, q_r)
         heads_out[...] = heads[...]
+        for copy in cache:
+            copy.wait()
+    for ph in range(2):
+        for n, pieces in enumerate((6, 14)):
+            remote(xs.at[ph, pl.ds(0, pieces)], xs.at[ph, pl.ds(0, pieces)], c_s.at[ph, n], c_r.at[ph, 0], x_peer).wait_send()
     for copy in waits:
         copy.wait_send()
 
@@ -479,17 +575,15 @@
     slab = pltpu.VMEM((GROUP, SEQS, HEAD), F32)
     dma = pltpu.SemaphoreType.DMA
     last = not following
-    hidden = jax.ShapeDtypeStruct((SEQS, MODEL), BF16)
+    hidden = kept((SEQS, MODEL), BF16)
     table = pltpu.VMEM((SEQS, HEAD), F32)
     return pl.pallas_call(
         functools.partial(mlp_kernel, layer, last),
-        out_shape=hidden if last else (hidden, jax.ShapeDtypeStruct(HEADS_SHAPE, F32)),
-        in_specs=[VM] * 8 + [ANY] * 3 + ([] if last else [SM, VM, VM, ANY]),
-        out_specs=VM if last else (VM, VM),
+        out_shape=hidden if last else (hidden, kept(HEADS_SHAPE, F32), CACHE, CACHE),
+        in_specs=[VM] * 8 + [HBM] * 3 + ([] if last else [HBM, VM, VM, HBM, HBM, HBM]),
+        out_specs=VM if last else (VM, VM, VM, VM),
         scratch_shapes=[
-            pltpu.VMEM((4, 1024, 512), BF16),
             pltpu.VMEM((UP_STEPS, MODEL, UP_N), BF16),
-            pltpu.VMEM((4, DOWN_K, 512), BF16),
             pltpu.VMEM((KVL, 2 * GROUP, HEAD), F32),
             pltpu.VMEM((3, 2 * GROUP, HEAD), F32),
             pltpu.VMEM((2, GROUP, SEQS, HEAD), F32),
@@ -504,11 +598,11 @@
             pltpu.VMEM((UP_STEPS, SEQS, 256), F32),
             pltpu.VMEM((SEQS, DOWN_K), BF16),
             pltpu.VMEM((4, SEQS, 512), F32),
-            dma((8 + UP_STEPS,)), dma((6,)), dma((6,)), dma((UP_STEPS,)), dma((UP_STEPS,)), dma((2, 20)), dma((2, 20)),
-        ] + ([] if last else [pltpu.VMEM(HEADS_SHAPE, F32), table, table, dma((6,)), dma((6,))]),
-        compiler_params=pltpu.CompilerParams(collective_id=2 + layer, has_side_effects=True, vmem_limit_bytes=63 * MIB),
+            dma((8 + UP_STEPS,)), dma((6,)), dma((6,)), dma((1,)), dma((1,)), dma((2, 2)), dma((2, 20)),
+        ] + ([] if last else [pltpu.SMEM((SEQS,), jnp.int32), pltpu.VMEM(HEADS_SHAPE, F32), table, table, dma((1,)), dma((2,)), dma((6,)), dma((6,))]),
+        compiler_params=pltpu.CompilerParams(collective_id=2 + layer, has_side_effects=True, vmem_limit_bytes=(60 if last else MLP_MIB) * MIB),
         name=f'mlp_{layer}',
-    )(o, ml, h, gain, shift, bd, bu, bn, wd, wu, wn, *following)
+    )(near(o), near(ml), near(h) if last else pin(h), *map(pin, (gain, shift, bd, bu, bn, wd, wu, wn, *following)))
 
 
 def solution(mesh):
@@ -524,13 +618,13 @@
         kc = k_cache.reshape(flat)
         vc = v_cache.reshape(flat)
         done = ()
-        heads = project(0, positions, freq, hidden, ln_gain, ln_bias, b_qkv, w_qkv)
+        heads, kb, vb = project(0, positions, freq, hidden, ln_gain, ln_bias, b_qkv, w_qkv, kc, vc)
         for layer in range(2):
-            ko, vo, o, ml = attend(layer, positions, heads.reshape(-1, HEAD), kc, vc, *done)
+            ko, vo, o, ml = attend(layer, positions, heads.reshape(-1, HEAD), kb, vb, flat, *done)
             done = (ko, vo)
-            following = () if layer else (positions, freq, b_qkv, w_qkv)
+            following = () if layer else (positions, freq, b_qkv, w_qkv, kc, vc)
             out = finish(layer, o.reshape(HEADS, SEQS, HEAD), ml, hidden, ln_gain, ln_bias, b_dense, b_up, b_down, w_dense, w_up, w_down, *following)
-            hidden, heads = out if following else (out, None)
+            hidden, heads, kb, vb = out if following else (out, None, None, None)
         return hidden, done[0].reshape(shape), done[1].reshape(shape)
 
     return jax.shard_map(device_step, mesh=mesh, in_specs=in_specs, out_specs=out_specs, check_vma=False)

time: 152 us -> 139 us (0.914)
  Pallas kernels: 149 us -> 138 us
    pallas_call x2, Pallas kernels: 28.8 us -> 17.7 us  [attend(): pl.pallas_call(functools.partial(attend_kernel, layer, layer == 0), out_s...]
where the time goes in v3:
time: 139 us
  Pallas kernels  138 us (99%)
    pallas_call x2, Pallas kernels, finish(): pl.pallas_call(functools.partial(mlp_kernel, layer, last), out_shape=hidd...  109 us
    pallas_call x2, Pallas kernels, attend(): pl.pallas_call(functools.partial(attend_kernel, layer, layer == 0), out_s...  17.7 us
    pallas_call x1, Pallas kernels, project(): pl.pallas_call(functools.partial(qkv_kernel, layer), out_shape=(kept(HEAD...  10.8 us

profile of v3, /device:TPU:0, one launch (start us, length us, event | category | flops | bytes accessed | tf_op | source)
XLA Modules:
  0.0 139.0 jit_solution(2573281991255649208)
XLA Ops:
  0.6 10.8 %qkv_0.1 = (f32[24,64,128]{2,1,0:T(8,128)S(1)}, bf16[64,512,128]{2,1,0:T(8,128)(2,1)S(1)}, bf16[64,512,128]{2,1,0:T(8,128)(2,1)S(1)}) custom-call(s32[64]{0:T(128)} %pos_hbm.5, f32[1,128]{1,0:T(1,128)} %constant.2.clone.freq_hbm.rest_1_, bf16[64,4096]{1,0:T(8,128)(2,1)} %h_ref.1, bf16[2,2,4096]{2,1,0:T(2,128)(2,1)} %gain_ref.3, ...), custom_call_target="tpu_custom_call" | custom-call | tf_op jit(solution)/shard_map/qkv_0/pallas_call | solution.py:181
  11.4 8.8 %attend_0.1 = (bf16[2,64,512,128]{3,2,1,0:T(8,128)(2,1)}, bf16[2,64,512,128]{3,2,1,0:T(8,128)(2,1)}, f32[1024,128]{1,0:T(8,128)S(1)}, f32[4,8,128]{2,1,0:T(8,128)S(1)}) custom-call(s32[64]{0:T(128)} %pos_hbm.5, f32[1536,128]{1,0:T(8,128)S(1)} %bitcast.8, bf16[64,512,128]{2,1,0:T(8,128)(2,1)S(1)} %get-tuple-element.19.kb, ...), custom_call_target="tpu_custom_call" | custom-call | tf_op jit(solution)/shard_map/attend_0/pallas_call | solution.py:303
  20.2 58.7 %mlp_0.1 = (bf16[64,4096]{1,0:T(8,128)(2,1)S(1)}, f32[24,64,128]{2,1,0:T(8,128)S(1)}, bf16[64,512,128]{2,1,0:T(8,128)(2,1)S(1)}, bf16[64,512,128]{2,1,0:T(8,128)(2,1)S(1)}) custom-call(f32[16,64,128]{2,1,0:T(8,128)S(1)} %bitcast.11, f32[4,8,128]{2,1,0:T(8,128)S(1)} %get-tuple-element.22.ml_ref, bf16[64,4096]{1,0:T(8,128)(2,1)} %h_ref.1, ...), custom_call_target="tpu_custom_call" | custom-call | tf_op jit(solution)/shard_map/mlp_0/pallas_call | solution.py:580
  79.0 8.8 %attend_1.1 = (bf16[2,64,512,128]{3,2,1,0:T(8,128)(2,1)}, bf16[2,64,512,128]{3,2,1,0:T(8,128)(2,1)}, f32[1024,128]{1,0:T(8,128)S(1)}, f32[4,8,128]{2,1,0:T(8,128)S(1)}) custom-call(s32[64]{0:T(128)} %pos_hbm.5, f32[1536,128]{1,0:T(8,128)S(1)} %bitcast.9, ...), custom_call_target="tpu_custom_call", output_to_operand_aliasing={{0}: (4, {}), {1}: (5, {})} | custom-call | tf_op jit(solution)/shard_map/attend_1/pallas_call | solution.py:303
  87.8 50.4 %mlp_1.1 = bf16[64,4096]{1,0:T(8,128)(2,1)S(1)} custom-call(f32[16,64,128]{2,1,0:T(8,128)S(1)} %bitcast.10, f32[4,8,128]{2,1,0:T(8,128)S(1)} %get-tuple-element.29.ml_ref, bf16[64,4096]{1,0:T(8,128)(2,1)S(1)} %get-tuple-element.30.h_ref, bf16[2,2,4096]{2,1,0:T(2,128)(2,1)} %gain_ref.3, bf16[2,2,4096]{2,1,0:T(2,128)(2,1)} %shift_ref.3, ...), custom_call_target="tpu_custom_call" | custom-call | tf_op jit(solution)/shard_map/mlp_1/pallas_call | solution.py:580
  138.2 0.8 copy.23

commit v4 on v3

v4 whole, which is shorter than its diff:
```python
import functools

import jax
import jax.numpy as jnp
import numpy as np
from jax import lax
from jax.experimental import pallas as pl
from jax.experimental.pallas import tpu as pltpu
from jax.sharding import PartitionSpec as P

BLOCK_SIZE = 64
LOCAL_BLOCKS = 16
VERT_STRIDE = 8
ROPE_THETA = 1000000.0
GELU_LIMIT = 20.0
NORM_EPS = 0.00001
MASKED = -1e30

SEQS = 64
MODEL = 4096
HEAD = 128
KVL = 4
GROUP = 4
HEADS = KVL * GROUP
SLOTS = 128
ROWS = SLOTS * KVL
QKV_N = (GROUP + 2) * HEAD
UP_N = 512
UP_STEPS = 7
DOWN_K = 3584
HALF_K = DOWN_K // 2
DENSE_K = 1024
OUT_STEPS = 4
PIECE = 256
CHUNK = 8
MIB = 1024 * 1024
QKV_MIB = 20
ATTEND_MIB = 8
MLP_MIB = 45

A, B = range(2)
K0, K1, K2, K3 = range(4)
A_FAR, B_FAR, A_X, B_Y, A_Y, B_X, A_LAST, B_LAST = range(12, 20)

F32 = jnp.float32
BF16 = jnp.bfloat16
MESH = pl.DeviceIdType.MESH
VM = pl.BlockSpec(memory_space=pltpu.VMEM)
SM = pl.BlockSpec(memory_space=pltpu.SMEM)
HBM = pl.BlockSpec(memory_space=pltpu.HBM)


def kept(shape, dtype):
    return pltpu.VMEM(shape, dtype)


def pin(x):
    return pltpu.with_memory_space_constraint(x, pltpu.HBM)


def near(x):
    return pltpu.with_memory_space_constraint(x, pltpu.VMEM)


def exchange(number, mib):
    return pltpu.CompilerParams(collective_id=number, has_side_effects=True, vmem_limit_bytes=mib * MIB)


def rowsum(a):
    return jnp.sum(a, axis=1, keepdims=True)


def block(index, size):
    return pl.ds(pl.multiple_of(index * size, size), size)


def dot(a, b):
    return jnp.dot(a, b, preferred_element_type=F32)


def place():
    sp = lax.axis_index('sp')
    return lax.axis_index('tp'), sp, sp // 2, lax.rem(sp, 2)


def enter(peers):
    barrier = pltpu.get_barrier_semaphore()
    for peer in peers:
        pl.semaphore_signal(barrier, inc=1, device_id=peer, device_id_type=MESH)
    pl.semaphore_wait(barrier, len(peers))


def remote(src, dst, send, recv, peer):
    return pltpu.make_async_remote_copy(src_ref=src, dst_ref=dst, send_sem=send, recv_sem=recv, device_id=peer, device_id_type=MESH)


def norm_into(pieces, gain, shift, out_ref):
    width = pieces[0]().shape[1]
    total = sum(rowsum(p()) for p in pieces)
    mean = total * (1.0 / MODEL)
    square = sum(rowsum(jnp.square(p() - mean)) for p in pieces)
    scale = lax.rsqrt(square * (1.0 / MODEL) + NORM_EPS)
    for i, p in enumerate(pieces):
        cols = slice(i * width, (i + 1) * width)
        out_ref[:, cols] = ((p() - mean) * scale * gain(cols) + shift(cols)).astype(BF16)


def position_rows(pos_ref, rows_ref):
    row = lax.broadcasted_iota(jnp.int32, (8, HEAD), 0)
    for first in range(0, SEQS, 8):
        pos = jnp.zeros((8, HEAD), jnp.int32)
        for i in range(8):
            pos = jnp.where(row == i, pos_ref[first + i], pos)
        rows_ref[first:first + 8] = pos


def rope_tables(rows_ref, freq_ref, cos_ref, sin_ref):
    sign = jnp.where(lax.broadcasted_iota(jnp.int32, (SEQS, HEAD), 1) < HEAD // 2, -1.0, 1.0)
    angle = rows_ref[...].astype(F32) * freq_ref[...]
    cos_ref[...] = jnp.cos(angle)
    sin_ref[...] = jnp.sin(angle) * sign


def load_qkv(layer, c, w_ref, wbuf, sem, j):
    cols = block(c * 3 + j, UP_N)
    return pltpu.make_async_copy(w_ref.at[layer, :, cols], wbuf.at[j], sem.at[j])


def qkv_phase(layer, c, partner, product, bias_ref, cos_ref, sin_ref, heads, ssem, rsem):
    sent = []
    for j in range(3):
        cols = block(c * 3 + j, UP_N)
        proj = product(j) + bias_ref[layer:layer + 1, cols].astype(F32)
        for n in range(4):
            local, i = divmod(4 * j + n, GROUP + 2)
            kv = 2 * c + local
            part = proj[:, n * HEAD:(n + 1) * HEAD]
            if i <= GROUP:
                part = part * cos_ref[...] + pltpu.roll(part, HEAD // 2, 1) * sin_ref[...]
            slot = kv * GROUP + i if i < GROUP else HEADS + (i - GROUP) * KVL + kv
            heads[slot] = part.astype(BF16).astype(F32)
            piece = {GROUP - 1: pl.ds(kv * GROUP, GROUP), GROUP: pl.ds(HEADS + kv, 1), GROUP + 1: pl.ds(HEADS + KVL + kv, 1)}.get(i)
            if piece is not None:
                k = len(sent)
                sent.append(remote(heads.at[piece], heads.at[piece], ssem.at[k], rsem.at[k], partner))
                sent[-1].start()
    for copy in sent:
        copy.wait()


def copy_in(pairs, sems):
    copies = [pltpu.make_async_copy(src, dst, sems.at[i]) for i, (src, dst) in enumerate(pairs)]
    for copy in copies:
        copy.start()
    return copies


def cache_copies(layer, kc_ref, vc_ref, k_out, v_out, sems):
    return [pltpu.make_async_copy(src.at[layer], dst, sems.at[n]) for n, (src, dst) in enumerate(((kc_ref, k_out), (vc_ref, v_out)))]


def qkv_kernel(
    layer, pos_hbm, freq_hbm, h_hbm, gain_hbm, shift_hbm, bias_hbm, w_ref, kc_ref, vc_ref, out_ref, k_out, v_out, rows_out,
    wbuf, u, heads, cos, sin, pos, freq, h, gain, shift, bias, isem, wsem, ksem, ssem, rsem,
):
    tp, sp, x, c = place()
    small = copy_in([(h_hbm, h), (gain_hbm, gain), (shift_hbm, shift), (pos_hbm, pos), (freq_hbm, freq), (bias_hbm, bias)], isem)
    loads = [load_qkv(layer, c, w_ref, wbuf, wsem, j) for j in range(3)]
    partner = {'sp': sp + 1 - 2 * c}
    for copy in small:
        copy.wait()

    def begin(j, _):
        load_qkv(layer, c, w_ref, wbuf, wsem, j).start()
        return 0

    lax.fori_loop(0, 3, begin, 0)
    for copy in cache_copies(layer, kc_ref, vc_ref, k_out, v_out, ksem):
        copy.start()
    norm_into(
        [lambda i=i: h[:, i * 512:(i + 1) * 512].astype(F32) for i in range(8)],
        lambda cols: gain[layer, 0:1, cols].astype(F32),
        lambda cols: shift[layer, 0:1, cols].astype(F32),
        u,
    )
    position_rows(pos, rows_out)
    rope_tables(rows_out, freq, cos, sin)
    enter([partner])

    def product(j):
        loads[j].wait()
        return dot(u[...], wbuf[j])

    qkv_phase(layer, c, partner, product, bias, cos, sin, heads, ssem, rsem)
    out_ref[...] = heads[...]
    for copy in cache_copies(layer, kc_ref, vc_ref, k_out, v_out, ksem):
        copy.wait()


HEADS_SHAPE = (HEADS + 2 * KVL, SEQS, HEAD)


CACHE = kept((SEQS, ROWS, HEAD), BF16)


def project(layer, positions, freq, h, gain, shift, bias, w, kc, vc):
    dma = pltpu.SemaphoreType.DMA
    return pl.pallas_call(
        functools.partial(qkv_kernel, layer),
        out_shape=(kept(HEADS_SHAPE, F32), CACHE, CACHE, kept((SEQS, HEAD), jnp.int32)),
        in_specs=[HBM] * 9,
        out_specs=(VM, VM, VM, VM),
        scratch_shapes=[
            pltpu.VMEM((3, MODEL, UP_N), BF16),
            pltpu.VMEM((SEQS, MODEL), BF16),
            pltpu.VMEM(HEADS_SHAPE, F32),
            pltpu.VMEM((SEQS, HEAD), F32),
            pltpu.VMEM((SEQS, HEAD), F32),
            pltpu.SMEM((SEQS,), jnp.int32),
            pltpu.VMEM((1, HEAD), F32),
            pltpu.VMEM((SEQS, MODEL), BF16),
            pltpu.VMEM(gain.shape, BF16),
            pltpu.VMEM(shift.shape, BF16),
            pltpu.VMEM(bias.shape, BF16),
            dma((6,)), dma((3,)), dma((2,)), dma((6,)), dma((6,)),
        ],
        compiler_params=exchange(layer, QKV_MIB),
        name=f'qkv_{layer}',
    )(*map(pin, (positions, freq, h, gain, shift, bias, w, kc, vc)))


def attend_kernel(layer, sparse, pos_hbm, heads_ref, kb, vb, *rest):
    if layer:
        rest = rest[2:]
    ko_ref, vo_ref, o_ref, ml_ref, pos_ref, mref, lref, slot_of, keep_of, tiles, psem, ssem, tsem = rest
    tp, sp, x, c = place()
    steps = SEQS // CHUNK
    copy_in([(pos_hbm, pos_ref)], psem)

    def save(i, n):
        dst, buf = ((ko_ref, kb), (vo_ref, vb))[n]
        rows = pl.ds(i * CHUNK, CHUNK)
        return pltpu.make_async_copy(buf.at[rows], dst.at[layer, rows], ssem.at[n, i])

    def place_of(b):
        t = pos_ref[b] - sp * SLOTS
        inside = jnp.logical_and(t >= 0, t < SLOTS)
        t = jnp.clip(t, 0, SLOTS - 1)
        return t, inside, pl.multiple_of((t // 4) * (4 * KVL), 4 * KVL)

    def patch(b, n):
        base = place_of(b)[2]
        return pltpu.make_async_copy(tiles.at[n, b], (ko_ref, vo_ref)[n].at[layer, b, pl.ds(base, 4 * KVL)], tsem.at[n])

    for i in range(steps):
        for n in range(2):
            save(i, n).start()
    row = lax.broadcasted_iota(jnp.int32, (HEADS, ROWS), 0)
    col = lax.broadcasted_iota(jnp.int32, (HEADS, ROWS), 1)
    slot = sp * SLOTS + col // KVL
    slot_of[...] = jnp.where(lax.rem(col, KVL) == row // GROUP, slot, jnp.int32(1 << 30))
    if sparse:
        block = slot // BLOCK_SIZE
        vertical = lax.rem(block + tp * HEADS + row + 1, VERT_STRIDE) == 0
        keep_of[...] = jnp.where(vertical, jnp.int32(1 << 20), block)
    mref[...] = jnp.zeros_like(mref)
    lref[...] = jnp.ones_like(lref)
    lane = lax.broadcasted_iota(jnp.int32, (HEADS, HEAD), 1)
    row16 = lax.broadcasted_iota(jnp.int32, (4 * KVL, HEAD), 0)

    pltpu.make_async_copy(pos_hbm, pos_ref, psem.at[0]).wait()

    def repeat(part):
        return jnp.concatenate([jnp.broadcast_to(part[kv:kv + 1], (GROUP, HEAD)) for kv in range(KVL)], axis=0)

    def body(i, _):
        for first in range(0, CHUNK, 4):
            ids = [i * CHUNK + first + s for s in range(4)]
            keeps, hits, scores, news = [], [], [], []
            for b in ids:
                q = heads_ref[pl.ds(b, HEADS, stride=SEQS), :]
                new = heads_ref[pl.ds(HEADS * SEQS + b, 2 * KVL, stride=SEQS), :]
                raw = lax.dot_general(q.astype(BF16), kb[b], (((1,), (1,)), ((), ())), preferred_element_type=F32)
                pos = pos_ref[b]
                keep = slot_of[...] <= pos
                hit = slot_of[...] == pos
                if sparse:
                    keep = jnp.logical_and(keep, pos // BLOCK_SIZE - keep_of[...] < LOCAL_BLOCKS)
                raw = jnp.where(hit, rowsum(q * repeat(new[:KVL])), raw)
                keeps.append(keep)
                hits.append(hit)
                news.append(new)
                scores.append(jnp.where(keep, raw * (1.0 / HEAD), MASKED))
            weights, added = [], []
            for b, keep, hit, score in zip(ids, keeps, hits, scores):
                peak = jnp.max(score, axis=1, keepdims=True)
                weight = jnp.where(keep, jnp.exp(score - peak), 0.0)
                mref[...] = jnp.where(lane == b, peak, mref[...])
                lref[...] = jnp.where(lane == b, rowsum(weight), lref[...])
                weight = weight.astype(BF16).astype(F32)
                added.append(rowsum(jnp.where(hit, weight, 0.0)))
                weights.append(jnp.where(hit, 0.0, weight).astype(BF16))
            for b, weight, extra, new in zip(ids, weights, added, news):
                o_ref[pl.ds(b, HEADS, stride=SEQS), :] = dot(weight, vb[b]) + extra * repeat(new[KVL:])
            for b, new in zip(ids, news):
                t, inside, base = place_of(b)
                hit = jnp.logical_and(row16 // KVL == lax.rem(t, 4), inside)
                for n, buf in enumerate((kb, vb)):
                    fresh = jnp.concatenate([new[n * KVL:(n + 1) * KVL]] * 4, axis=0)
                    tiles[n, b] = jnp.where(hit, fresh, buf[b, pl.ds(base, 4 * KVL), :].astype(F32)).astype(BF16)
        for n in range(2):
            save(i, n).wait()
        for s in range(CHUNK):
            for n in range(2):
                patch(i * CHUNK + s, n).start()
        return 0

    lax.fori_loop(0, steps, body, 0)
    for kv in range(KVL):
        ml_ref[kv, 0:GROUP] = mref[kv * GROUP:(kv + 1) * GROUP]
        ml_ref[kv, GROUP:2 * GROUP] = lref[kv * GROUP:(kv + 1) * GROUP]

    for n in range(2):
        pltpu.make_async_copy(tiles.at[n], (ko_ref, vo_ref)[n].at[layer, :, pl.ds(0, 4 * KVL)], tsem.at[n]).wait()


def attend(layer, positions, heads, kb, vb, shape, *done):
    cache = jax.ShapeDtypeStruct(shape, BF16)
    dma = pltpu.SemaphoreType.DMA
    return pl.pallas_call(
        functools.partial(attend_kernel, layer, layer == 0),
        out_shape=(cache, cache, kept((HEADS * SEQS, HEAD), F32), kept((KVL, 2 * GROUP, HEAD), F32)),
        in_specs=[HBM, VM, VM, VM] + [HBM] * len(done),
        out_specs=(HBM, HBM, VM, VM),
        scratch_shapes=[
            pltpu.SMEM((SEQS,), jnp.int32),
            pltpu.VMEM((HEADS, HEAD), F32),
            pltpu.VMEM((HEADS, HEAD), F32),
            pltpu.VMEM((HEADS, ROWS), jnp.int32),
            pltpu.VMEM((HEADS, ROWS), jnp.int32),
            pltpu.VMEM((2, SEQS, 4 * KVL, HEAD), BF16),
            dma((1,)), dma((2, SEQS // CHUNK)), dma((2,)),
        ],
        input_output_aliases={4: 0, 5: 1} if done else {},
        compiler_params=pltpu.CompilerParams(vmem_limit_bytes=ATTEND_MIB * MIB),
        name=f'attend_{layer}',
    )(pin(positions), *map(near, (heads, kb, vb)), *map(pin, done))


def mlp_kernel(layer, last, ahead, o_ref, ml_ref, h_ref, gain_ref, shift_ref, bd_ref, bu_ref, bn_ref, wd_ref, wu_ref, wn_ref, *rest):
    if not last:
        rows_ref, freq_ref, bq_ref, wq_ref, kc_ref, vc_ref, out_ref, heads_out, k_out, v_out = rest[:10]
        heads, cos, sin, k_s, q_s, q_r = rest[-6:]
        rest = rest[10:-6]
    else:
        out_ref, rest = rest[0], rest[1:]
    (
        wu, wn, mls, mlx, fromcore, tosend, kept, fromx, mine, other, ob, part, ra, rb, xs, u, mf, mp, mb, ps, acc, st, mo,
        wsem, o_s, o_r, m_s, m_r, c_s, c_r, t_s, t_r,
    ) = rest
    tp, sp, x, c = place()
    y = tp
    core_peer = {'sp': sp + 1 - 2 * c}
    x_peer = {'sp': 2 * (1 - x) + 1 - c}
    y_peer = {'tp': 1 - tp, 'sp': 2 * x + 1 - c}
    c = lax.rem(c + x + y, 2)
    oc, ox, oy = 1 - c, 1 - x, 1 - y
    quarter = [2 * ox + oy, 2 * ox + y, 2 * x + oy, 2 * x + y]

    def turn(k):
        far, near = 1 - k // 2, k // 2
        return 2 * (far * ox + near * x) + (1 - k % 2) * oy + k % 2 * y

    def cols_of(k):
        return block(c * 4 + turn(k), UP_N)

    def load_dense(k):
        return pltpu.make_async_copy(wd_ref.at[layer, block(x, DENSE_K), cols_of(k)], wu.at[UP_STEPS - 1, pl.ds(k * DENSE_K, DENSE_K)], wsem.at[k])

    def load_up(j):
        cols = block((2 * x + c) * UP_STEPS + j, UP_N)
        return pltpu.make_async_copy(wu_ref.at[layer, :, cols], wu.at[j], wsem.at[4 + j])

    def load_down(k):
        rows = block(x, DOWN_K)
        to = wn.at[k] if k < ahead else wu.at[k - ahead, pl.ds(0, DOWN_K)]
        return pltpu.make_async_copy(wn_ref.at[layer, rows, cols_of(k)], to, wsem.at[4 + UP_STEPS + k])

    def down_half(k, half):
        rows = block(half, HALF_K)
        return dot(mb[:, rows], wn[k, rows] if k < ahead else wu[k - ahead, rows])

    def load_next(j):
        return load_qkv(layer + 1, c, wq_ref, wu.at[pl.ds(4, 3)], wsem, j)

    for k in range(OUT_STEPS):
        load_dense(k).start()
    for j in range(UP_STEPS - 1):
        load_up(j).start()
    for k in range(ahead):
        load_down(k).start()
    if not last:
        cache = cache_copies(layer + 1, kc_ref, vc_ref, k_out, v_out, k_s)
        for copy in cache:
            copy.start()
    everyone = [lax.rem(tp * 4 + sp + r, 8) for r in range(1, 8)]
    enter([{'tp': peer // 4, 'sp': lax.rem(peer, 4)} for peer in everyone])
    waits = []

    def swap(i, src, dst, peer):
        copy = remote(src, dst, o_s.at[i], o_r.at[i], peer)
        copy.start()
        waits.append(copy)
        return copy

    stats = swap(4, ml_ref, mls, core_peer)
    slabs = [None, None]
    for n, xd in enumerate((ox, x)):
        src = o_ref.at[pl.ds((2 * xd + oc) * GROUP, GROUP)]
        slabs[n] = swap(n, src, fromcore.at[n], core_peer)

    def columns(rows):
        return jnp.concatenate(rows + [jnp.zeros((HEAD - GROUP * len(rows), HEAD), F32)], axis=0).T[:SEQS]

    def merge(one, two):
        top = jnp.maximum(one[:GROUP], two[:GROUP])
        first, second = jnp.exp(one[:GROUP] - top), jnp.exp(two[:GROUP] - top)
        return first, second, top, first * one[GROUP:] + second * two[GROUP:]

    stats.wait_recv()
    rows = []
    for n, xd in enumerate((ox, x)):
        first, second, top, total = merge(ml_ref[2 * xd + c], mls[2 * xd + c])
        rows += [first, second]
        mlx[n] = jnp.concatenate([top, total], axis=0)
    cross_ml = swap(5, mlx.at[0], mlx.at[2], x_peer)
    scale = columns(rows)
    for n, (xd, out) in enumerate(((ox, tosend), (x, kept))):
        slabs[n].wait_recv()
        kv = 2 * xd + c
        for g in range(GROUP):
            i = 2 * n * GROUP + g
            out[g] = o_ref[kv * GROUP + g] * scale[:, i:i + 1] + fromcore[n, g] * scale[:, i + GROUP:i + GROUP + 1]
        if n == 0:
            cross = swap(2, tosend, fromx, x_peer)
    if not last:
        rope_tables(rows_ref, freq_ref, cos, sin)
    cross_ml.wait_recv()
    first, second, _, total = merge(mlx[1], mlx[2])
    scale = columns([first / total, second / total])
    cross.wait_recv()
    for g in range(GROUP):
        val = (kept[g] * scale[:, g:g + 1] + fromx[g] * scale[:, g + GROUP:g + GROUP + 1]).astype(BF16)
        mine[g] = val.astype(F32)
        ob[:, block(c * GROUP + g, HEAD)] = val
    share = swap(3, mine, other, core_peer)
    def dense_half(k, half):
        return dot(ob[:, block(half, UP_N)], wu[UP_STEPS - 1, block(2 * k + half, UP_N)])

    for k in range(OUT_STEPS):
        load_dense(k).wait()
        ps[k] = dense_half(k, c)
    share.wait_recv()
    for g in range(GROUP):
        ob[:, block(oc * GROUP + g, HEAD)] = other[g].astype(BF16)

    own = (c * 4 + quarter[K3]) * 2

    def all_reduce(ph, chunk, residual, bias_ref, after=lambda: None, stats=True):
        def post(i, src, dst, peer):
            copy = remote(src, dst, c_s.at[ph, int(i > 5)], c_r.at[ph, i], peer)
            copy.start()
            return copy

        def keep(k):
            val = chunk(k)
            part[ph, k, A] = val[:, :PIECE]
            part[ph, k, B] = val[:, PIECE:]

        keep(K0)
        a0 = post(0, part.at[ph, K0, A], ra.at[ph, K0], x_peer)
        b0 = post(1, part.at[ph, K0, B], rb.at[ph, K0], y_peer)
        keep(K1)
        a1 = post(2, part.at[ph, K1, A], ra.at[ph, K1], x_peer)
        keep(K2)
        b1 = post(3, part.at[ph, K2, B], rb.at[ph, K1], y_peer)
        keep(K3)
        after()
        b0.wait_recv()
        part[ph, K1, B] += rb[ph, K0]
        b2 = post(4, part.at[ph, K1, B], rb.at[ph, K2], x_peer)
        a0.wait_recv()
        part[ph, K2, A] += ra[ph, K0]
        a2 = post(5, part.at[ph, K2, A], ra.at[ph, K2], y_peer)
        for half, (first, second, landed) in enumerate(((a1, a2, ra), (b1, b2, rb))):
            first.wait_recv()
            second.wait_recv()
            cols = block(own + half, PIECE)
            full = part[ph, K3, half] + landed[ph, K1] + landed[ph, K2]
            xs[ph, own + half] = (residual(half, cols) + full + bias_ref[layer:layer + 1, cols].astype(F32)).astype(BF16).astype(F32)
        if stats:
            send_moments(ph)
        gather = {}
        for n in range(3):
            for half in range(2):
                peer = core_peer if n == 2 else (x_peer, y_peer)[(n + half) % 2]
                mine_ref = xs.at[ph, own + half]
                gather[half, n] = post(6 + 3 * half + n, mine_ref, mine_ref, peer)
        base = c * 8
        from_x = base + quarter[K1] * 2
        from_y = base + quarter[K2] * 2
        far = base + quarter[K0] * 2

        def forward(i, piece, peer):
            ref = xs.at[ph, piece]
            return post(i, ref, ref, peer)

        sent = {}

        def pump(step):
            if step == 0:
                gather[A, K0].wait_recv()
                sent[A_FAR] = forward(A_FAR, from_x, y_peer)
                sent[A_X] = forward(A_X, from_x, core_peer)
                gather[B, K0].wait_recv()
                sent[B_FAR] = forward(B_FAR, from_y + 1, x_peer)
                sent[B_Y] = forward(B_Y, from_y + 1, core_peer)
            elif step == 1:
                gather[A, K1].wait_recv()
                sent[A_Y] = forward(A_Y, from_y, core_peer)
                gather[B, K1].wait_recv()
                sent[B_X] = forward(B_X, from_x + 1, core_peer)
            else:
                sent[A_FAR].wait_recv()
                sent[A_LAST] = forward(A_LAST, far, core_peer)
                sent[B_FAR].wait_recv()
                sent[B_LAST] = forward(B_LAST, far + 1, core_peer)

        def arrive(group):
            for copy in {0: [gather[A, K2], gather[B, K2]], 1: [sent.get(i) for i in (A_X, B_Y, A_Y, B_X)], 2: [sent.get(i) for i in (A_LAST, B_LAST)]}[group]:
                copy.wait_recv()

        return pump, arrive

    me = tp * 4 + sp

    def send_moments(ph):
        a, b = xs[ph, own], xs[ph, own + 1]
        count = 2 * PIECE
        mean = (rowsum(a) + rowsum(b)) * (1.0 / count)
        spread = rowsum(jnp.square(a - mean)) + rowsum(jnp.square(b - mean))
        lane = lax.broadcasted_iota(jnp.int32, (SEQS, HEAD), 1)
        both = jnp.where(lane == 0, mean, jnp.where(lane == 1, spread, 0.0))
        st[ph, me] = jnp.concatenate([both, jnp.zeros((HEAD - SEQS, HEAD), F32)], axis=0).T[:8]
        for r in range(1, 8):
            peer = lax.rem(me + r, 8)
            remote(st.at[ph, me], st.at[ph, me], t_s.at[ph], t_r.at[ph], {'tp': peer // 4, 'sp': lax.rem(peer, 4)}).start()

    def moments(ph):
        remote(st.at[ph, pl.ds(0, 7)], st.at[ph, pl.ds(0, 7)], t_s.at[ph], t_r.at[ph], x_peer).wait()
        parts = [st[ph, i] for i in range(8)]
        mean = sum(p[0:1] for p in parts) * 0.125
        spread = sum(p[1:2] + (2.0 * PIECE) * jnp.square(p[0:1] - mean) for p in parts)
        scale = lax.rsqrt(spread * (1.0 / MODEL) + NORM_EPS)
        table = jnp.concatenate([mean, scale, jnp.zeros((HEAD - 2, HEAD), F32)], axis=0).T[:SEQS]
        mo[...] = table

    def slices(group):
        if group == 0:
            return c * 4 + quarter[K3], oc * 4 + quarter[K3]
        if group == 2:
            return c * 4 + quarter[K0], oc * 4 + quarter[K0]
        return [core * 4 + quarter[k] for core in (c, oc) for k in (1, 2)]

    def norm_group(ph, row, norm, group):
        mean, scale = mo[:, 0:1], mo[:, 1:2]
        for n, index in enumerate(slices(group)):
            for half in range(2):
                cols = block(2 * index + half, PIECE)
                gain, shift = gain_ref[row, norm:norm + 1, cols].astype(F32), shift_ref[row, norm:norm + 1, cols].astype(F32)
                at = (2 * n + half) * PIECE
                u[:, at:at + PIECE] = ((xs[ph, 2 * index + half] - mean) * scale * gain + shift).astype(BF16)

    def product(group, slot):
        total = 0.0
        for n, index in enumerate(slices(group)):
            rows = block(index, UP_N)
            total = total + dot(u[:, n * 512:(n + 1) * 512], wu[slot, rows])
        return total

    def normed_product(ph, row, norm, stages, first, count, wait, finish_step):
        pump, arrive = stages

        def add(group, low, high):
            def step(j, _):
                if group == 0:
                    wait(j)
                    acc[j] = product(group, first + j)
                else:
                    acc[j] += product(group, first + j)
                return 0

            lax.fori_loop(low, high, step, 0, unroll=True)

        half = count // 2 + 1
        moments(ph)
        arrive(0)
        norm_group(ph, row, norm, 0)
        pump(0)
        add(0, 0, half)
        pump(1)
        add(0, half, count)
        arrive(1)
        norm_group(ph, row, norm, 1)
        add(1, 0, half)
        pump(2)
        add(1, half, count)
        arrive(2)
        norm_group(ph, row, norm, 2)
        finish_step(lambda j: acc[j] + product(2, first + j))

    def dense_chunk(k):
        return ps[k] + dense_half(k, oc)

    stages = all_reduce(0, dense_chunk, lambda half, cols: h_ref[:, cols].astype(F32), bd_ref, load_up(UP_STEPS - 1).start)
    take = (lax.broadcasted_iota(jnp.int32, (2 * HEAD, HEAD), 0) == 2 * lax.broadcasted_iota(jnp.int32, (2 * HEAD, HEAD), 1)).astype(BF16)
    even = lax.rem(lax.broadcasted_iota(jnp.int32, (SEQS, UP_N), 1), 2) == 0

    def share_m(j):
        return remote(mf.at[j], mp.at[j], m_s.at[0], m_r.at[0], core_peer)

    def up_step(full, j):
        cols = block((2 * x + c) * UP_STEPS + j, UP_N)
        val = full(j) + bu_ref[layer:layer + 1, cols].astype(F32)
        gate = jnp.minimum(val, GELU_LIMIT)
        gate = gate * (1.0 / (1.0 + jnp.exp(-1.702 * gate)))
        linear = jnp.clip(val, -GELU_LIMIT, GELU_LIMIT) + 1.0
        mixed = jnp.where(even, gate * pltpu.roll(linear, UP_N - 1, 1), 0.0).astype(BF16)
        packed = jnp.concatenate([dot(mixed[:, i:i + 2 * HEAD], take) for i in range(0, UP_N, 2 * HEAD)], axis=1)
        mf[j] = packed
        share_m(j).start()
        mb[:, block(c * UP_STEPS + j, PIECE)] = packed.astype(BF16)

        if j < 4 - ahead:
            load_down(j + ahead).start()
        if not last and j >= 4:
            load_next(j - 4).start()

    def up_steps(full):
        for j in range(UP_STEPS):
            up_step(full, j)

    normed_product(0, layer, 1, stages, 0, UP_STEPS, lambda j: load_up(j).wait(), up_steps)
    for k in range(OUT_STEPS):
        load_down(k).wait()
        ps[k] = down_half(k, c)
    remote(mf, mp, m_s.at[0], m_r.at[0], core_peer).wait()
    for j in range(UP_STEPS):
        mb[:, block(oc * UP_STEPS + j, PIECE)] = mp[j].astype(BF16)

    def down_chunk(k):
        return ps[k] + down_half(k, oc)

    stages = all_reduce(1, down_chunk, lambda half, cols: xs[0, own + half], bn_ref, stats=not last)
    if last:
        pump, arrive = stages
        for step in range(3):
            pump(step)
        for group in range(3):
            arrive(group)
    else:
        def qkv_steps(full):
            qkv_phase(layer + 1, c, core_peer, full, bq_ref, cos, sin, heads, q_s, q_r)

        normed_product(1, layer + 1, 0, stages, 4, 3, lambda j: load_next(j).wait(), qkv_steps)
        heads_out[...] = heads[...]
        for copy in cache:
            copy.wait()
    for i in range(16):
        out_ref[:, i * PIECE:(i + 1) * PIECE] = xs[1, i].astype(BF16)
    for ph in range(2):
        for n, pieces in enumerate((6, 14)):
            remote(xs.at[ph, pl.ds(0, pieces)], xs.at[ph, pl.ds(0, pieces)], c_s.at[ph, n], c_r.at[ph, 0], x_peer).wait_send()
    for copy in waits:
        copy.wait_send()


def finish(layer, o, ml, h, gain, shift, bd, bu, bn, wd, wu, wn, *following):
    slab = pltpu.VMEM((GROUP, SEQS, HEAD), F32)
    dma = pltpu.SemaphoreType.DMA
    last = not following
    ahead = 4 if last else 1
    hidden = kept((SEQS, MODEL), BF16)
    table = pltpu.VMEM((SEQS, HEAD), F32)
    return pl.pallas_call(
        functools.partial(mlp_kernel, layer, last, ahead),
        out_shape=hidden if last else (hidden, kept(HEADS_SHAPE, F32), CACHE, CACHE),
        in_specs=[VM] * 8 + [HBM] * 3 + ([] if last else [VM, VM, VM, HBM, HBM, HBM]),
        out_specs=VM if last else (VM, VM, VM, VM),
        scratch_shapes=[
            pltpu.VMEM((UP_STEPS, MODEL, UP_N), BF16),
            pltpu.VMEM((ahead, DOWN_K, 512), BF16),
            pltpu.VMEM((KVL, 2 * GROUP, HEAD), F32),
            pltpu.VMEM((3, 2 * GROUP, HEAD), F32),
            pltpu.VMEM((2, GROUP, SEQS, HEAD), F32),
            slab, slab, slab, slab, slab,
            pltpu.VMEM((SEQS, 1024), BF16),
            pltpu.VMEM((2, 4, 2, SEQS, PIECE), F32),
            pltpu.VMEM((2, 3, SEQS, PIECE), F32),
            pltpu.VMEM((2, 3, SEQS, PIECE), F32),
            pltpu.VMEM((2, 16, SEQS, PIECE), F32),
            pltpu.VMEM((SEQS, 2048), BF16),
            pltpu.VMEM((UP_STEPS, SEQS, 256), F32),
            pltpu.VMEM((UP_STEPS, SEQS, 256), F32),
            pltpu.VMEM((SEQS, DOWN_K), BF16),
            pltpu.VMEM((4, SEQS, 512), F32),
            pltpu.VMEM((UP_STEPS, SEQS, UP_N), F32),
            pltpu.VMEM((2, 8, 8, HEAD), F32),
            pltpu.VMEM((SEQS, HEAD), F32),
            dma((8 + UP_STEPS,)), dma((6,)), dma((6,)), dma((1,)), dma((1,)), dma((2, 2)), dma((2, 20)), dma((2,)), dma((2,)),
        ] + ([] if last else [pltpu.VMEM(HEADS_SHAPE, F32), table, table, dma((2,)), dma((6,)), dma((6,))]),
        compiler_params=exchange(2 + layer, (60 if last else MLP_MIB)),
        name=f'mlp_{layer}',
    )(near(o), near(ml), near(h) if last else pin(h), *map(pin, (gain, shift, bd, bu, bn, wd, wu, wn)), *map(near, following[:1]), *map(pin, following[1:]))


def solution(mesh):
    cache_spec = P(None, 'dp', 'sp', 'tp', None)
    rows, bias, cols = P(None, 'tp', None), P(None, 'tp'), P(None, None, 'tp')
    in_specs = (P('dp'), P('dp'), cache_spec, cache_spec, P(), P(), cols, bias, rows, P(), cols, bias, rows, P())
    out_specs = (P('dp'), cache_spec, cache_spec)

    def device_step(hidden, positions, k_cache, v_cache, ln_gain, ln_bias, w_qkv, b_qkv, w_dense, b_dense, w_up, b_up, w_down, b_down):
        freq = ROPE_THETA ** (-np.arange(HEAD // 2) * (2.0 / HEAD))
        freq = jnp.asarray(np.tile(freq, 2)[None].astype(np.float32))
        shape = k_cache.shape
        flat = (2, SEQS, ROWS, HEAD)
        kc = k_cache.reshape(flat)
        vc = v_cache.reshape(flat)
        done = ()
        heads, kb, vb, rows = project(0, positions, freq, hidden, ln_gain, ln_bias, b_qkv, w_qkv, kc, vc)
        for layer in range(2):
            ko, vo, o, ml = attend(layer, positions, heads.reshape(-1, HEAD), kb, vb, flat, *done)
            done = (ko, vo)
            following = () if layer else (rows, freq, b_qkv, w_qkv, kc, vc)
            out = finish(layer, o.reshape(HEADS, SEQS, HEAD), ml, hidden, ln_gain, ln_bias, b_dense, b_up, b_down, w_dense, w_up, w_down, *following)
            hidden, heads, kb, vb = out if following else (out, None, None, None)
        return hidden, done[0].reshape(shape), done[1].reshape(shape)

    return jax.shard_map(device_step, mesh=mesh, in_specs=in_specs, out_specs=out_specs, check_vma=False)
```

time: 139 us -> 130 us (0.935)
  Pallas kernels: 138 us -> 128 us
    pallas_call x2, Pallas kernels: 109 us -> 99.8 us  [finish(): pl.pallas_call(functools.partial(mlp_kernel, layer, last, ahead), out_sha...]
where the time goes in v4:
time: 130 us
  Pallas kernels  128 us (98%)
    pallas_call x2, Pallas kernels, finish(): pl.pallas_call(functools.partial(mlp_kernel, layer, last, ahead), out_sha...  99.8 us
    pallas_call x2, Pallas kernels, attend(): pl.pallas_call(functools.partial(attend_kernel, layer, layer == 0), out_s...  17.8 us
    pallas_call x1, Pallas kernels, project(): pl.pallas_call(functools.partial(qkv_kernel, layer), out_shape=(kept(HEAD...  10.8 us

profile of v4, /device:TPU:0, one launch (start us, length us, event | category | flops | bytes accessed | tf_op | source)
XLA Modules:
  0.0 129.9 jit_solution(17805034158040375921)
XLA Ops:
  0.6 10.8 %qkv_0.1 = (f32[24,64,128]{2,1,0:T(8,128)S(1)}, bf16[64,512,128]{2,1,0:T(8,128)(2,1)S(1)}, bf16[64,512,128]{2,1,0:T(8,128)(2,1)S(1)}, s32[64,128]{1,0:T(8,128)S(1)}) custom-call(s32[64]{0:T(128)} %pos_hbm.5, f32[1,128]{1,0:T(1,128)} %constant.2.clone.freq_hbm.rest_1_, bf16[64,4096]{1,0:T(8,128)(2,1)} %h_ref.1, bf16[2,2,4096]{2,1,0:T(2,128)(2,1)} %gain_ref.3, ...), custom_call_target="tpu_custom_call" | custom-call | tf_op jit(solution)/shard_map/qkv_0/pallas_call | solution.py:208
  11.4 8.8 %attend_0.1 = (bf16[2,64,512,128]{3,2,1,0:T(8,128)(2,1)}, bf16[2,64,512,128]{3,2,1,0:T(8,128)(2,1)}, f32[1024,128]{1,0:T(8,128)S(1)}, f32[4,8,128]{2,1,0:T(8,128)S(1)}) custom-call(s32[64]{0:T(128)} %pos_hbm.5, f32[1536,128]{1,0:T(8,128)S(1)} %bitcast.8, bf16[64,512,128]{2,1,0:T(8,128)(2,1)S(1)} %get-tuple-element.20.kb, ...), custom_call_target="tpu_custom_call" | custom-call | tf_op jit(solution)/shard_map/attend_0/pallas_call | solution.py:330
  20.2 53.5 %mlp_0.1 = (bf16[64,4096]{1,0:T(8,128)(2,1)S(1)}, f32[24,64,128]{2,1,0:T(8,128)S(1)}, bf16[64,512,128]{2,1,0:T(8,128)(2,1)S(1)}, bf16[64,512,128]{2,1,0:T(8,128)(2,1)S(1)}) custom-call(f32[16,64,128]{2,1,0:T(8,128)S(1)} %bitcast.11, f32[4,8,128]{2,1,0:T(8,128)S(1)} %get-tuple-element.23.ml_ref, bf16[64,4096]{1,0:T(8,128)(2,1)} %h_ref.1, ...), custom_call_target="tpu_custom_call" | custom-call | tf_op jit(solution)/shard_map/mlp_0/pallas_call | solution.py:695
  73.7 9.0 %attend_1.1 = (bf16[2,64,512,128]{3,2,1,0:T(8,128)(2,1)}, bf16[2,64,512,128]{3,2,1,0:T(8,128)(2,1)}, f32[1024,128]{1,0:T(8,128)S(1)}, f32[4,8,128]{2,1,0:T(8,128)S(1)}) custom-call(s32[64]{0:T(128)} %pos_hbm.5, f32[1536,128]{1,0:T(8,128)S(1)} %bitcast.9, ...), custom_call_target="tpu_custom_call", output_to_operand_aliasing={{0}: (4, {}), {1}: (5, {})} | custom-call | tf_op jit(solution)/shard_map/attend_1/pallas_call | solution.py:330
  82.7 46.3 %mlp_1.1 = bf16[64,4096]{1,0:T(8,128)(2,1)S(1)} custom-call(f32[16,64,128]{2,1,0:T(8,128)S(1)} %bitcast.10, f32[4,8,128]{2,1,0:T(8,128)S(1)} %get-tuple-element.31.ml_ref, bf16[64,4096]{1,0:T(8,128)(2,1)S(1)} %get-tuple-element.32.h_ref, bf16[2,2,4096]{2,1,0:T(2,128)(2,1)} %gain_ref.3, bf16[2,2,4096]{2,1,0:T(2,128)(2,1)} %shift_ref.3, ...), custom_call_target="tpu_custom_call" | custom-call | tf_op jit(solution)/shard_map/mlp_1/pallas_call | solution.py:695
  129.1 0.8 copy.23

commit v5 on v4

--- a/solution.py
+++ b/solution.py
@@ -40,7 +40,12 @@
 
 A, B = range(2)
 K0, K1, K2, K3 = range(4)
-A_FAR, B_FAR, A_X, B_Y, A_Y, B_X, A_LAST, B_LAST = range(12, 20)
+STRIP = 20
+LATE_SEQS = 16
+EARLY = pl.ds(0, SEQS - LATE_SEQS)
+LATE = pl.ds(SEQS - LATE_SEQS, LATE_SEQS)
+STRIPS = (pl.ds(0, HEAD), pl.ds(HEAD, HEAD))
+A_FAR, B_FAR, A_X, B_Y, A_Y, B_X, A_LAST, B_LAST = range(12, STRIP)
 
 F32 = jnp.float32
 BF16 = jnp.bfloat16
@@ -126,7 +131,7 @@
     return pltpu.make_async_copy(w_ref.at[layer, :, cols], wbuf.at[j], sem.at[j])
 
 
-def qkv_phase(layer, c, partner, product, bias_ref, cos_ref, sin_ref, heads, ssem, rsem):
+def qkv_phase(layer, c, partner, product, bias_ref, cos_ref, sin_ref, heads, ssem, rsem, meanwhile=lambda: None):
     sent = []
     for j in range(3):
         cols = block(c * 3 + j, UP_N)
@@ -144,6 +149,7 @@
                 k = len(sent)
                 sent.append(remote(heads.at[piece], heads.at[piece], ssem.at[k], rsem.at[k], partner))
                 sent[-1].start()
+    meanwhile()
     for copy in sent:
         copy.wait()
 
@@ -155,8 +161,8 @@
     return copies
 
 
-def cache_copies(layer, kc_ref, vc_ref, k_out, v_out, sems):
-    return [pltpu.make_async_copy(src.at[layer], dst, sems.at[n]) for n, (src, dst) in enumerate(((kc_ref, k_out), (vc_ref, v_out)))]
+def cache_copies(layer, kc_ref, vc_ref, k_out, v_out, sems, rows=pl.ds(0, SEQS)):
+    return [pltpu.make_async_copy(src.at[layer, rows], dst.at[pl.ds(0, rows.size)], sems.at[n]) for n, (src, dst) in enumerate(((kc_ref, k_out), (vc_ref, v_out)))]
 
 
 def qkv_kernel(
@@ -175,7 +181,7 @@
         return 0
 
     lax.fori_loop(0, 3, begin, 0)
-    for copy in cache_copies(layer, kc_ref, vc_ref, k_out, v_out, ksem):
+    for copy in cache_copies(layer, kc_ref, vc_ref, k_out, v_out, ksem, EARLY):
         copy.start()
     norm_into(
         [lambda i=i: h[:, i * 512:(i + 1) * 512].astype(F32) for i in range(8)],
@@ -193,7 +199,7 @@
 
     qkv_phase(layer, c, partner, product, bias, cos, sin, heads, ssem, rsem)
     out_ref[...] = heads[...]
-    for copy in cache_copies(layer, kc_ref, vc_ref, k_out, v_out, ksem):
+    for copy in cache_copies(layer, kc_ref, vc_ref, k_out, v_out, ksem, EARLY):
         copy.wait()
 
 
@@ -230,17 +236,15 @@
 
 
 def attend_kernel(layer, sparse, pos_hbm, heads_ref, kb, vb, *rest):
-    if layer:
-        rest = rest[2:]
-    ko_ref, vo_ref, o_ref, ml_ref, pos_ref, mref, lref, slot_of, keep_of, tiles, psem, ssem, tsem = rest
+    aside, rest = rest[:2], rest[2:]
+    ko_ref, vo_ref, o_ref, ml_ref, pos_ref, mref, lref, slot_of, keep_of, tiles, psem, ssem, tsem, *late = rest
+    early = SEQS - LATE_SEQS if late else SEQS
     tp, sp, x, c = place()
     steps = SEQS // CHUNK
     copy_in([(pos_hbm, pos_ref)], psem)
 
-    def save(i, n):
-        dst, buf = ((ko_ref, kb), (vo_ref, vb))[n]
-        rows = pl.ds(i * CHUNK, CHUNK)
-        return pltpu.make_async_copy(buf.at[rows], dst.at[layer, rows], ssem.at[n, i])
+    def save(bufs, skip, i, n):
+        return pltpu.make_async_copy(bufs[n].at[pl.ds(i * CHUNK - skip, CHUNK)], (ko_ref, vo_ref)[n].at[layer, pl.ds(i * CHUNK, CHUNK)], ssem.at[n, i])
 
     def place_of(b):
         t = pos_ref[b] - sp * SLOTS
@@ -252,9 +256,14 @@
         base = place_of(b)[2]
         return pltpu.make_async_copy(tiles.at[n, b], (ko_ref, vo_ref)[n].at[layer, b, pl.ds(base, 4 * KVL)], tsem.at[n])
 
-    for i in range(steps):
+    if late:
+        lk, lv, late_sem = late
+        late_loads = cache_copies(layer, *aside, lk, lv, late_sem, LATE)
+        for copy in late_loads:
+            copy.start()
+    for i in range(early // CHUNK):
         for n in range(2):
-            save(i, n).start()
+            save((kb, vb), 0, i, n).start()
     row = lax.broadcasted_iota(jnp.int32, (HEADS, ROWS), 0)
     col = lax.broadcasted_iota(jnp.int32, (HEADS, ROWS), 1)
     slot = sp * SLOTS + col // KVL
@@ -273,14 +282,15 @@
     def repeat(part):
         return jnp.concatenate([jnp.broadcast_to(part[kv:kv + 1], (GROUP, HEAD)) for kv in range(KVL)], axis=0)
 
-    def body(i, _):
+    def body(bufs, skip, i, _):
+        kb, vb = bufs
         for first in range(0, CHUNK, 4):
             ids = [i * CHUNK + first + s for s in range(4)]
             keeps, hits, scores, news = [], [], [], []
             for b in ids:
                 q = heads_ref[pl.ds(b, HEADS, stride=SEQS), :]
                 new = heads_ref[pl.ds(HEADS * SEQS + b, 2 * KVL, stride=SEQS), :]
-                raw = lax.dot_general(q.astype(BF16), kb[b], (((1,), (1,)), ((), ())), preferred_element_type=F32)
+                raw = lax.dot_general(q.astype(BF16), kb[b - skip], (((1,), (1,)), ((), ())), preferred_element_type=F32)
                 pos = pos_ref[b]
                 keep = slot_of[...] <= pos
                 hit = slot_of[...] == pos
@@ -301,21 +311,28 @@
                 added.append(rowsum(jnp.where(hit, weight, 0.0)))
                 weights.append(jnp.where(hit, 0.0, weight).astype(BF16))
             for b, weight, extra, new in zip(ids, weights, added, news):
-                o_ref[pl.ds(b, HEADS, stride=SEQS), :] = dot(weight, vb[b]) + extra * repeat(new[KVL:])
+                o_ref[pl.ds(b, HEADS, stride=SEQS), :] = dot(weight, vb[b - skip]) + extra * repeat(new[KVL:])
             for b, new in zip(ids, news):
                 t, inside, base = place_of(b)
                 hit = jnp.logical_and(row16 // KVL == lax.rem(t, 4), inside)
                 for n, buf in enumerate((kb, vb)):
                     fresh = jnp.concatenate([new[n * KVL:(n + 1) * KVL]] * 4, axis=0)
-                    tiles[n, b] = jnp.where(hit, fresh, buf[b, pl.ds(base, 4 * KVL), :].astype(F32)).astype(BF16)
+                    tiles[n, b] = jnp.where(hit, fresh, buf[b - skip, pl.ds(base, 4 * KVL), :].astype(F32)).astype(BF16)
         for n in range(2):
-            save(i, n).wait()
+            save(bufs, skip, i, n).wait()
         for s in range(CHUNK):
             for n in range(2):
                 patch(i * CHUNK + s, n).start()
         return 0
 
-    lax.fori_loop(0, steps, body, 0)
+    lax.fori_loop(0, early // CHUNK, functools.partial(body, (kb, vb), 0), 0)
+    if late:
+        for copy in late_loads:
+            copy.wait()
+        for i in range(early // CHUNK, steps):
+            for n in range(2):
+                save((lk, lv), early, i, n).start()
+        lax.fori_loop(early // CHUNK, steps, functools.partial(body, (lk, lv), early), 0)
     for kv in range(KVL):
         ml_ref[kv, 0:GROUP] = mref[kv * GROUP:(kv + 1) * GROUP]
         ml_ref[kv, GROUP:2 * GROUP] = lref[kv * GROUP:(kv + 1) * GROUP]
@@ -324,13 +341,13 @@
         pltpu.make_async_copy(tiles.at[n], (ko_ref, vo_ref)[n].at[layer, :, pl.ds(0, 4 * KVL)], tsem.at[n]).wait()
 
 
-def attend(layer, positions, heads, kb, vb, shape, *done):
+def attend(layer, positions, heads, kb, vb, shape, *aside):
     cache = jax.ShapeDtypeStruct(shape, BF16)
     dma = pltpu.SemaphoreType.DMA
     return pl.pallas_call(
         functools.partial(attend_kernel, layer, layer == 0),
         out_shape=(cache, cache, kept((HEADS * SEQS, HEAD), F32), kept((KVL, 2 * GROUP, HEAD), F32)),
-        in_specs=[HBM, VM, VM, VM] + [HBM] * len(done),
+        in_specs=[HBM, VM, VM, VM, HBM, HBM],
         out_specs=(HBM, HBM, VM, VM),
         scratch_shapes=[
             pltpu.SMEM((SEQS,), jnp.int32),
@@ -340,11 +357,11 @@
             pltpu.VMEM((HEADS, ROWS), jnp.int32),
             pltpu.VMEM((2, SEQS, 4 * KVL, HEAD), BF16),
             dma((1,)), dma((2, SEQS // CHUNK)), dma((2,)),
-        ],
-        input_output_aliases={4: 0, 5: 1} if done else {},
+        ] + ([] if layer else [pltpu.VMEM((LATE_SEQS, ROWS, HEAD), BF16)] * 2 + [dma((2,))]),
+        input_output_aliases={4: 0, 5: 1} if layer else {},
         compiler_params=pltpu.CompilerParams(vmem_limit_bytes=ATTEND_MIB * MIB),
         name=f'attend_{layer}',
-    )(pin(positions), *map(near, (heads, kb, vb)), *map(pin, done))
+    )(pin(positions), *map(near, (heads, kb, vb)), *map(pin, aside))
 
 
 def mlp_kernel(layer, last, ahead, o_ref, ml_ref, h_ref, gain_ref, shift_ref, bd_ref, bu_ref, bn_ref, wd_ref, wu_ref, wn_ref, *rest):
@@ -468,7 +485,7 @@
 
     def all_reduce(ph, chunk, residual, bias_ref, after=lambda: None, stats=True):
         def post(i, src, dst, peer):
-            copy = remote(src, dst, c_s.at[ph, int(i > 5)], c_r.at[ph, i], peer)
+            copy = remote(src, dst, c_s.at[ph, int(5 < i < STRIP)], c_r.at[ph, i], peer)
             copy.start()
             return copy
 
@@ -477,24 +494,31 @@
             part[ph, k, A] = val[:, :PIECE]
             part[ph, k, B] = val[:, PIECE:]
 
+        def strips(i, src, dst, peer):
+            return [post((i, i + STRIP)[n], src.at[:, cols], dst.at[:, cols], peer) for n, cols in enumerate(STRIPS)]
+
         keep(K0)
-        a0 = post(0, part.at[ph, K0, A], ra.at[ph, K0], x_peer)
-        b0 = post(1, part.at[ph, K0, B], rb.at[ph, K0], y_peer)
+        a0 = strips(0, part.at[ph, K0, A], ra.at[ph, K0], x_peer)
+        b0 = strips(1, part.at[ph, K0, B], rb.at[ph, K0], y_peer)
         keep(K1)
         a1 = post(2, part.at[ph, K1, A], ra.at[ph, K1], x_peer)
         keep(K2)
         b1 = post(3, part.at[ph, K2, B], rb.at[ph, K1], y_peer)
         keep(K3)
         after()
-        b0.wait_recv()
-        part[ph, K1, B] += rb[ph, K0]
-        b2 = post(4, part.at[ph, K1, B], rb.at[ph, K2], x_peer)
-        a0.wait_recv()
-        part[ph, K2, A] += ra[ph, K0]
-        a2 = post(5, part.at[ph, K2, A], ra.at[ph, K2], y_peer)
+        a2, b2 = [], []
+        for n, cols in enumerate(STRIPS):
+            b0[n].wait_recv()
+            part[ph, K1, B, :, cols] += rb[ph, K0, :, cols]
+            ref = part.at[ph, K1, B, :, cols]
+            b2.append(post((4, 4 + STRIP)[n], ref, rb.at[ph, K2, :, cols], x_peer))
+            a0[n].wait_recv()
+            part[ph, K2, A, :, cols] += ra[ph, K0, :, cols]
+            ref = part.at[ph, K2, A, :, cols]
+            a2.append(post((5, 5 + STRIP)[n], ref, ra.at[ph, K2, :, cols], y_peer))
         for half, (first, second, landed) in enumerate(((a1, a2, ra), (b1, b2, rb))):
-            first.wait_recv()
-            second.wait_recv()
+            for copy in (first, *second):
+                copy.wait_recv()
             cols = block(own + half, PIECE)
             full = part[ph, K3, half] + landed[ph, K1] + landed[ph, K2]
             xs[ph, own + half] = (residual(half, cols) + full + bias_ref[layer:layer + 1, cols].astype(F32)).astype(BF16).astype(F32)
@@ -662,22 +686,28 @@
         return ps[k] + down_half(k, oc)
 
     stages = all_reduce(1, down_chunk, lambda half, cols: xs[0, own + half], bn_ref, stats=not last)
+    def write(group):
+        for index in slices(group):
+            for half in range(2):
+                out_ref[:, block(2 * index + half, PIECE)] = xs[1, 2 * index + half].astype(BF16)
+
     if last:
         pump, arrive = stages
-        for step in range(3):
-            pump(step)
         for group in range(3):
-            arrive(group)
+            pump(group)
+            if group:
+                arrive(group - 1)
+                write(group - 1)
+        arrive(2)
+        write(2)
     else:
         def qkv_steps(full):
-            qkv_phase(layer + 1, c, core_peer, full, bq_ref, cos, sin, heads, q_s, q_r)
+            qkv_phase(layer + 1, c, core_peer, full, bq_ref, cos, sin, heads, q_s, q_r, lambda: [write(group) for group in range(3)])
 
         normed_product(1, layer + 1, 0, stages, 4, 3, lambda j: load_next(j).wait(), qkv_steps)
         heads_out[...] = heads[...]
         for copy in cache:
             copy.wait()
-    for i in range(16):
-        out_ref[:, i * PIECE:(i + 1) * PIECE] = xs[1, i].astype(BF16)
     for ph in range(2):
         for n, pieces in enumerate((6, 14)):
             remote(xs.at[ph, pl.ds(0, pieces)], xs.at[ph, pl.ds(0, pieces)], c_s.at[ph, n], c_r.at[ph, 0], x_peer).wait_send()
@@ -717,7 +747,7 @@
             pltpu.VMEM((UP_STEPS, SEQS, UP_N), F32),
             pltpu.VMEM((2, 8, 8, HEAD), F32),
             pltpu.VMEM((SEQS, HEAD), F32),
-            dma((8 + UP_STEPS,)), dma((6,)), dma((6,)), dma((1,)), dma((1,)), dma((2, 2)), dma((2, 20)), dma((2,)), dma((2,)),
+            dma((8 + UP_STEPS,)), dma((6,)), dma((6,)), dma((1,)), dma((1,)), dma((2, 2)), dma((2, STRIP + 6)), dma((2,)), dma((2,)),
         ] + ([] if last else [pltpu.VMEM(HEADS_SHAPE, F32), table, table, dma((2,)), dma((6,)), dma((6,))]),
         compiler_params=exchange(2 + layer, (60 if last else MLP_MIB)),
         name=f'mlp_{layer}',
@@ -740,7 +770,7 @@
         done = ()
         heads, kb, vb, rows = project(0, positions, freq, hidden, ln_gain, ln_bias, b_qkv, w_qkv, kc, vc)
         for layer in range(2):
-            ko, vo, o, ml = attend(layer, positions, heads.reshape(-1, HEAD), kb, vb, flat, *done)
+            ko, vo, o, ml = attend(layer, positions, heads.reshape(-1, HEAD), kb, vb, flat, *(done or (kc, vc)))
             done = (ko, vo)
             following = () if layer else (rows, freq, b_qkv, w_qkv, kc, vc)
             out = finish(layer, o.reshape(HEADS, SEQS, HEAD), ml, hidden, ln_gain, ln_bias, b_dense, b_up, b_down, w_dense, w_up, w_down, *following)

time: 130 us -> 127 us (0.977)
  Pallas kernels: 128 us -> 126 us
    pallas_call x2, Pallas kernels: 99.8 us -> 97.9 us  [finish(): pl.pallas_call(functools.partial(mlp_kernel, layer, last, ahead), out_sha...]
where the time goes in v5:
time: 127 us
  Pallas kernels  126 us (99%)
    pallas_call x2, Pallas kernels, finish(): pl.pallas_call(functools.partial(mlp_kernel, layer, last, ahead), out_sha...  97.9 us
    pallas_call x2, Pallas kernels, attend(): pl.pallas_call(functools.partial(attend_kernel, layer, layer == 0), out_s...  18.2 us
    pallas_call x1, Pallas kernels, project(): pl.pallas_call(functools.partial(qkv_kernel, layer), out_shape=(kept(HEAD...  9.56 us

profile of v5, /device:TPU:0, one launch (start us, length us, event | category | flops | bytes accessed | tf_op | source)
XLA Modules:
  0.0 127.2 jit_solution(7045019561658931026)
XLA Ops:
  0.6 9.6 %qkv_0.1 = (f32[24,64,128]{2,1,0:T(8,128)S(1)}, bf16[64,512,128]{2,1,0:T(8,128)(2,1)S(1)}, bf16[64,512,128]{2,1,0:T(8,128)(2,1)S(1)}, s32[64,128]{1,0:T(8,128)S(1)}) custom-call(s32[64]{0:T(128)} %pos_hbm.5, f32[1,128]{1,0:T(1,128)} %constant.2.clone.freq_hbm.rest_1_, bf16[64,4096]{1,0:T(8,128)(2,1)} %h_ref.1, bf16[2,2,4096]{2,1,0:T(2,128)(2,1)} %gain_ref.3, ...), custom_call_target="tpu_custom_call" | custom-call | tf_op jit(solution)/shard_map/qkv_0/pallas_call | solution.py:214
  10.2 9.4 %attend_0.1 = (bf16[2,64,512,128]{3,2,1,0:T(8,128)(2,1)}, bf16[2,64,512,128]{3,2,1,0:T(8,128)(2,1)}, f32[1024,128]{1,0:T(8,128)S(1)}, f32[4,8,128]{2,1,0:T(8,128)S(1)}) custom-call(s32[64]{0:T(128)} %pos_hbm.5, f32[1536,128]{1,0:T(8,128)S(1)} %bitcast.9, bf16[64,512,128]{2,1,0:T(8,128)(2,1)S(1)} %get-tuple-element.20.kb, ...), custom_call_target="tpu_custom_call" | custom-call | tf_op jit(solution)/shard_map/attend_0/pallas_call | solution.py:347
  19.6 52.4 %mlp_0.1 = (bf16[64,4096]{1,0:T(8,128)(2,1)S(1)}, f32[24,64,128]{2,1,0:T(8,128)S(1)}, bf16[64,512,128]{2,1,0:T(8,128)(2,1)S(1)}, bf16[64,512,128]{2,1,0:T(8,128)(2,1)S(1)}) custom-call(f32[16,64,128]{2,1,0:T(8,128)S(1)} %bitcast.11, f32[4,8,128]{2,1,0:T(8,128)S(1)} %get-tuple-element.23.ml_ref, bf16[64,4096]{1,0:T(8,128)(2,1)} %h_ref.1, ...), custom_call_target="tpu_custom_call" | custom-call | tf_op jit(solution)/shard_map/mlp_0/pallas_call | solution.py:725
  72.0 8.8 %attend_1.1 = (bf16[2,64,512,128]{3,2,1,0:T(8,128)(2,1)}, bf16[2,64,512,128]{3,2,1,0:T(8,128)(2,1)}, f32[1024,128]{1,0:T(8,128)S(1)}, f32[4,8,128]{2,1,0:T(8,128)S(1)}) custom-call(s32[64]{0:T(128)} %pos_hbm.5, f32[1536,128]{1,0:T(8,128)S(1)} %bitcast.8, ...), custom_call_target="tpu_custom_call", output_to_operand_aliasing={{0}: (4, {}), {1}: (5, {})} | custom-call | tf_op jit(solution)/shard_map/attend_1/pallas_call | solution.py:347
  80.8 45.5 %mlp_1.1 = bf16[64,4096]{1,0:T(8,128)(2,1)S(1)} custom-call(f32[16,64,128]{2,1,0:T(8,128)S(1)} %bitcast.10, f32[4,8,128]{2,1,0:T(8,128)S(1)} %get-tuple-element.31.ml_ref, bf16[64,4096]{1,0:T(8,128)(2,1)S(1)} %get-tuple-element.32.h_ref, bf16[2,2,4096]{2,1,0:T(2,128)(2,1)} %gain_ref.3, bf16[2,2,4096]{2,1,0:T(2,128)(2,1)} %shift_ref.3, ...), custom_call_target="tpu_custom_call" | custom-call | tf_op jit(solution)/shard_map/mlp_1/pallas_call | solution.py:725
  126.4 0.8 copy.23

commit v6 on v5

--- a/solution.py
+++ b/solution.py
@@ -36,7 +36,7 @@
 MIB = 1024 * 1024
 QKV_MIB = 20
 ATTEND_MIB = 8
-MLP_MIB = 45
+MLP_MIB = 43
 
 A, B = range(2)
 K0, K1, K2, K3 = range(4)
@@ -561,7 +561,7 @@
                 sent[B_LAST] = forward(B_LAST, far + 1, core_peer)
 
         def arrive(group):
-            for copy in {0: [gather[A, K2], gather[B, K2]], 1: [sent.get(i) for i in (A_X, B_Y, A_Y, B_X)], 2: [sent.get(i) for i in (A_LAST, B_LAST)]}[group]:
+            for copy in {0: [gather[A, K2], gather[B, K2]], 2: [sent.get(i) for i in (A_X, B_Y, A_Y, B_X)], 3: [sent.get(i) for i in (A_LAST, B_LAST)]}.get(group, ()):
                 copy.wait_recv()
 
         return pump, arrive
@@ -590,11 +590,9 @@
         mo[...] = table
 
     def slices(group):
-        if group == 0:
-            return c * 4 + quarter[K3], oc * 4 + quarter[K3]
-        if group == 2:
-            return c * 4 + quarter[K0], oc * 4 + quarter[K0]
-        return [core * 4 + quarter[k] for core in (c, oc) for k in (1, 2)]
+        if group in (0, 3):
+            return [core * 4 + quarter[K0 if group else K3] for core in (c, oc)]
+        return [(oc if group == 2 else c) * 4 + quarter[k] for k in (K1, K2)]
 
     def norm_group(ph, row, norm, group):
         mean, scale = mo[:, 0:1], mo[:, 1:2]
@@ -634,14 +632,15 @@
         add(0, 0, half)
         pump(1)
         add(0, half, count)
-        arrive(1)
-        norm_group(ph, row, norm, 1)
-        add(1, 0, half)
-        pump(2)
-        add(1, half, count)
-        arrive(2)
-        norm_group(ph, row, norm, 2)
-        finish_step(lambda j: acc[j] + product(2, first + j))
+        for group in (1, 2):
+            arrive(group)
+            norm_group(ph, row, norm, group)
+            add(group, 0, count)
+            if group == 1:
+                pump(2)
+        arrive(3)
+        norm_group(ph, row, norm, 3)
+        finish_step(lambda j: acc[j] + product(3, first + j))
 
     def dense_chunk(k):
         return ps[k] + dense_half(k, oc)
@@ -693,16 +692,15 @@
 
     if last:
         pump, arrive = stages
-        for group in range(3):
-            pump(group)
-            if group:
-                arrive(group - 1)
-                write(group - 1)
-        arrive(2)
-        write(2)
+        for step in range(3):
+            pump(step)
+            arrive(step)
+            write(step)
+        arrive(3)
+        write(3)
     else:
         def qkv_steps(full):
-            qkv_phase(layer + 1, c, core_peer, full, bq_ref, cos, sin, heads, q_s, q_r, lambda: [write(group) for group in range(3)])
+            qkv_phase(layer + 1, c, core_peer, full, bq_ref, cos, sin, heads, q_s, q_r, lambda: [write(group) for group in range(4)])
 
         normed_product(1, layer + 1, 0, stages, 4, 3, lambda j: load_next(j).wait(), qkv_steps)
         heads_out[...] = heads[...]
@@ -739,7 +737,7 @@
             pltpu.VMEM((2, 3, SEQS, PIECE), F32),
             pltpu.VMEM((2, 3, SEQS, PIECE), F32),
             pltpu.VMEM((2, 16, SEQS, PIECE), F32),
-            pltpu.VMEM((SEQS, 2048), BF16),
+            pltpu.VMEM((SEQS, 1024), BF16),
             pltpu.VMEM((UP_STEPS, SEQS, 256), F32),
             pltpu.VMEM((UP_STEPS, SEQS, 256), F32),
             pltpu.VMEM((SEQS, DOWN_K), BF16),
@@ -749,9 +747,9 @@
             pltpu.VMEM((SEQS, HEAD), F32),
             dma((8 + UP_STEPS,)), dma((6,)), dma((6,)), dma((1,)), dma((1,)), dma((2, 2)), dma((2, STRIP + 6)), dma((2,)), dma((2,)),
         ] + ([] if last else [pltpu.VMEM(HEADS_SHAPE, F32), table, table, dma((2,)), dma((6,)), dma((6,))]),
-        compiler_params=exchange(2 + layer, (60 if last else MLP_MIB)),
+        compiler_params=exchange(2 + layer, 54 if last else MLP_MIB),
         name=f'mlp_{layer}',
-    )(near(o), near(ml), near(h) if last else pin(h), *map(pin, (gain, shift, bd, bu, bn, wd, wu, wn)), *map(near, following[:1]), *map(pin, following[1:]))
+    )(near(o), near(ml), near(h) if last else pin(h), *map(near, (gain, shift, bd, bu, bn)), *map(pin, (wd, wu, wn)), *map(near, following[:1]), *map(pin, following[1:]))
 
 
 def solution(mesh):

time: 127 us -> 126 us (level)
  Pallas kernels: 126 us -> 124 us
    pallas_call x2, Pallas kernels: 97.9 us -> 96.5 us  [finish(): pl.pallas_call(functools.partial(mlp_kernel, layer, last, ahead), out_sha...]
where the time goes in v6:
time: 126 us
  Pallas kernels  124 us (98%)
    pallas_call x2, Pallas kernels, finish(): pl.pallas_call(functools.partial(mlp_kernel, layer, last, ahead), out_sha...  96.5 us
    pallas_call x2, Pallas kernels, attend(): pl.pallas_call(functools.partial(attend_kernel, layer, layer == 0), out_s...  18.2 us
    pallas_call x1, Pallas kernels, project(): pl.pallas_call(functools.partial(qkv_kernel, layer), out_shape=(kept(HEAD...  9.56 us

profile of v6, /device:TPU:0, one launch (start us, length us, event | category | flops | bytes accessed | tf_op | source)
XLA Modules:
  0.0 125.9 jit_solution(8568718008892140402)
XLA Ops:
  0.6 9.6 %qkv_0.1 = (f32[24,64,128]{2,1,0:T(8,128)S(1)}, bf16[64,512,128]{2,1,0:T(8,128)(2,1)S(1)}, bf16[64,512,128]{2,1,0:T(8,128)(2,1)S(1)}, s32[64,128]{1,0:T(8,128)S(1)}) custom-call(s32[64]{0:T(128)} %pos_hbm.5, f32[1,128]{1,0:T(1,128)} %constant.2.clone.freq_hbm.rest_1_, bf16[64,4096]{1,0:T(8,128)(2,1)} %h_ref.1, bf16[2,2,4096]{2,1,0:T(2,128)(2,1)} %gain_ref.3, ...), custom_call_target="tpu_custom_call" | custom-call | tf_op jit(solution)/shard_map/qkv_0/pallas_call | solution.py:214
  10.2 0.0 copy-start
  10.2 0.0 copy-start.1
  10.2 0.0 copy-start.2
  10.2 0.0 copy-start.3
  10.2 0.0 copy-start.4
  10.3 9.4 %attend_0.1 = (bf16[2,64,512,128]{3,2,1,0:T(8,128)(2,1)}, bf16[2,64,512,128]{3,2,1,0:T(8,128)(2,1)}, f32[1024,128]{1,0:T(8,128)S(1)}, f32[4,8,128]{2,1,0:T(8,128)S(1)}) custom-call(s32[64]{0:T(128)} %pos_hbm.5, f32[1536,128]{1,0:T(8,128)S(1)} %bitcast.9, bf16[64,512,128]{2,1,0:T(8,128)(2,1)S(1)} %get-tuple-element.20.kb, ...), custom_call_target="tpu_custom_call" | custom-call | tf_op jit(solution)/shard_map/attend_0/pallas_call | solution.py:347
  19.6 0.0 copy-done
  19.7 0.0 copy-done.1
  19.7 0.0 copy-done.2
  19.7 0.0 copy-done.3
  19.7 0.0 copy-done.4
  19.7 52.2 %mlp_0.1 = (bf16[64,4096]{1,0:T(8,128)(2,1)S(1)}, f32[24,64,128]{2,1,0:T(8,128)S(1)}, bf16[64,512,128]{2,1,0:T(8,128)(2,1)S(1)}, bf16[64,512,128]{2,1,0:T(8,128)(2,1)S(1)}) custom-call(f32[16,64,128]{2,1,0:T(8,128)S(1)} %bitcast.11, f32[4,8,128]{2,1,0:T(8,128)S(1)} %get-tuple-element.23.ml_ref, bf16[64,4096]{1,0:T(8,128)(2,1)} %h_ref.1, ...), custom_call_target="tpu_custom_call" | custom-call | tf_op jit(solution)/shard_map/mlp_0/pallas_call | solution.py:723
  71.9 8.8 %attend_1.1 = (bf16[2,64,512,128]{3,2,1,0:T(8,128)(2,1)}, bf16[2,64,512,128]{3,2,1,0:T(8,128)(2,1)}, f32[1024,128]{1,0:T(8,128)S(1)}, f32[4,8,128]{2,1,0:T(8,128)S(1)}) custom-call(s32[64]{0:T(128)} %pos_hbm.5, f32[1536,128]{1,0:T(8,128)S(1)} %bitcast.8, ...), custom_call_target="tpu_custom_call", output_to_operand_aliasing={{0}: (4, {}), {1}: (5, {})} | custom-call | tf_op jit(solution)/shard_map/attend_1/pallas_call | solution.py:347
  80.8 44.3 %mlp_1.1 = bf16[64,4096]{1,0:T(8,128)(2,1)S(1)} custom-call(f32[16,64,128]{2,1,0:T(8,128)S(1)} %bitcast.10, f32[4,8,128]{2,1,0:T(8,128)S(1)} %get-tuple-element.31.ml_ref, bf16[64,4096]{1,0:T(8,128)(2,1)S(1)} %get-tuple-element.32.h_ref, bf16[2,2,4096]{2,1,0:T(2,128)(2,1)S(1)} %copy-done, bf16[2,2,4096]{2,1,0:T(2,128)(2,1)S(1)} %copy-done.1, ...), custom_call_target="tpu_custom_call" | custom-call | tf_op jit(solution)/shard_map/mlp_1/pallas_call | solution.py:723
  125.1 0.8 copy.23
Async XLA Ops:
  10.2 9.5 %copy-start = (bf16[2,2,4096]{2,1,0:T(2,128)(2,1)S(1)}, bf16[2,2,4096]{2,1,0:T(2,128)(2,1)}, u32[]{:S(2)}) copy-start(bf16[2,2,4096]{2,1,0:T(2,128)(2,1)} %gain_ref.3) | copy-start | bytes 98308
  10.2 9.5 %copy-start.1 = (bf16[2,2,4096]{2,1,0:T(2,128)(2,1)S(1)}, bf16[2,2,4096]{2,1,0:T(2,128)(2,1)}, u32[]{:S(2)}) copy-start(bf16[2,2,4096]{2,1,0:T(2,128)(2,1)} %shift_ref.3) | copy-start | bytes 98308
  10.2 9.4 %copy-start.2 = (bf16[2,14336]{1,0:T(2,128)(2,1)S(1)}, bf16[2,14336]{1,0:T(2,128)(2,1)}, u32[]{:S(2)}) copy-start(bf16[2,14336]{1,0:T(2,128)(2,1)} %bu_ref.3) | copy-start | bytes 172036
  10.2 9.4 %copy-start.3 = (bf16[2,4096]{1,0:T(2,128)(2,1)S(1)}, bf16[2,4096]{1,0:T(2,128)(2,1)}, u32[]{:S(2)}) copy-start(bf16[2,4096]{1,0:T(2,128)(2,1)} %bd_ref.3) | copy-start | bytes 49156
  10.2 9.4 %copy-start.4 = (bf16[2,4096]{1,0:T(2,128)(2,1)S(1)}, bf16[2,4096]{1,0:T(2,128)(2,1)}, u32[]{:S(2)}) copy-start(bf16[2,4096]{1,0:T(2,128)(2,1)} %bn_ref.3) | copy-start | bytes 49156
